TPU v7x, 32 devices: a whole 2x2x4 slice. The times are simulated.
32 devices in a mesh: gx: 4 (over z), gy: 4 (over y, x), gz: 2 (over core).
Axes of the slice: x: 2, y: 2, z: 4, core: 2. Of those that a mesh axis runs over, the one named last changes fastest.
Arguments:
- volume: float32 [32, 256, 4096], P('gz', 'gy', 'gx'), may hold values from -24 to 24
Outputs:
- level_one: float32 [16, 128, 2048], P('gz', 'gy', 'gx')
- level_two: float32 [8, 64, 1024], P('gz', 'gy', 'gx')
- level_three: float32 [4, 32, 512], P('gz', 'gy', 'gx')
All inputs are finite; a program needn't handle non-finite values.
Results may differ from a plain program's by a relative error of at most 0.00002.
Values sent between devices are 32-bit elements; how exact they have to be, the bound alone decides.
A program may use at most 64 MiB of HBM per device.

v0:
```python
import functools

import jax
import jax.numpy as jnp
from jax import lax
from jax.experimental import pallas as pl
from jax.experimental.pallas import tpu as pltpu
from jax.sharding import PartitionSpec as P

LANES = 128
MESH = pl.DeviceIdType.MESH
AXES = ("gz", "gy", "gx")
W0, W1, W2 = 0.0625, 0.25, 0.375


def taps_of(delta):
    far = jnp.abs(delta)
    return jnp.where(
        far == 0, W2, jnp.where(far == 1, W1, jnp.where(far == 2, W0, 0.0))
    ).astype(jnp.bfloat16)


def column_weights():
    row = lax.broadcasted_iota(jnp.int32, (LANES, LANES), 0)
    col = lax.broadcasted_iota(jnp.int32, (LANES, LANES), 1)
    before = taps_of(row - LANES - 2 * col)
    first = taps_of(row - 2 * col)
    second = taps_of(row + LANES - 2 * col)
    after = taps_of(row + 2 * LANES - 2 * col)
    half = LANES // 2
    signed_in = jnp.where(row < half, row, row - LANES)
    signed_out = jnp.where(col < half, col, col - LANES)
    same_side = (row < half) == (col < half)
    halo = taps_of(jnp.where(same_side, signed_in - 2 * signed_out, LANES))
    return before, first, second, after, halo


def split3(x):
    hi = x.astype(jnp.bfloat16)
    rest = x - hi.astype(jnp.float32)
    mid = rest.astype(jnp.bfloat16)
    lo = (rest - mid.astype(jnp.float32)).astype(jnp.bfloat16)
    return hi, mid, lo


def dots(parts, weights):
    total = None
    for p in (2, 1, 0):
        lhs = jnp.concatenate([q[p] for q in parts], axis=1)
        d = jnp.dot(lhs, weights, preferred_element_type=jnp.float32)
        total = d if total is None else total + d
    return total


def kernel(sizes, dims, vol, out1, out2, out3,
           v, z, t, sh, rz_lo, rz_hi, ys_lo, ys_hi, yr_lo, yr_hi, xs, xr, wm, wh,
           load_sem, zsend, zrecv, ysend, yrecv, xsend, xrecv):
    nz, ny, nt = dims
    idx = {a: lax.axis_index(a) for a in AXES}
    has = {}
    near = {}
    for a in AXES:
        has[a, -1], has[a, 1] = idx[a] > 0, idx[a] < sizes[a] - 1
        near[a, -1] = jnp.maximum(idx[a] - 1, 0)
        near[a, 1] = jnp.minimum(idx[a] + 1, sizes[a] - 1)

    def flag(a, d):
        return jnp.where(has[a, d], 1.0, 0.0).astype(jnp.float32)

    def exists(steps):
        found = None
        for a, d in steps.items():
            found = has[a, d] if found is None else jnp.logical_and(found, has[a, d])
        return found

    def device(steps):
        return {a: near[a, d] for a, d in steps.items()}

    step = 16 if ny % 16 == 0 else 8
    groups = [(r, step) for r in range(0, ny, step)]
    loads = []
    for g, (r0, rn) in enumerate(groups):
        c = pltpu.make_async_copy(
            vol.at[:, pl.ds(r0, rn), :], v.at[:, pl.ds(r0, rn), :], load_sem.at[g])
        c.start()
        loads.append(c)

    xr[...] = jnp.zeros(xr.shape, jnp.float32)
    for lev in range(3):
        yr_lo[lev][...] = jnp.zeros(yr_lo[lev].shape, jnp.float32)
        yr_hi[lev][...] = jnp.zeros(yr_hi[lev].shape, jnp.float32)

    corners = [{"gz": i, "gy": j} for i in (-1, 1) for j in (-1, 1)]
    peers = [{a: d} for a in AXES for d in (-1, 1)] + corners
    barrier = pltpu.get_barrier_semaphore()
    for p in peers:
        @pl.when(exists(p))
        def _():
            pl.semaphore_signal(barrier, inc=1, device_id=device(p), device_id_type=MESH)

    for lev in range(3):
        pad = z[lev].shape[:2]
        rows = z[lev].shape[2] - 32
        first_pad = 8 + rows if lev == 0 else 16 + rows
        if lev == 0:
            z[lev][:, :, 0:8, :] = jnp.zeros(pad + (8, LANES), jnp.float32)
        z[lev][:, :, first_pad:32 + rows, :] = jnp.zeros(
            pad + (32 + rows - first_pad, LANES), jnp.float32)
    before, first, second, after, halo = column_weights()
    for i, m in enumerate((before, first, second, after)):
        wm[i * LANES:(i + 1) * LANES] = m
    for i, m in enumerate((before, halo, after)):
        wh[i * LANES:(i + 1) * LANES] = m

    sent = []

    def send(steps, src, dst, send_sem, recv_sem):
        copy = pltpu.make_async_remote_copy(
            src_ref=src, dst_ref=dst, send_sem=send_sem, recv_sem=recv_sem,
            device_id=device(steps), device_id_type=MESH)

        @pl.when(exists(steps))
        def _():
            copy.start()
        sent.append((steps, copy))

        def wait():
            @pl.when(exists({a: -d for a, d in steps.items()}))
            def _():
                copy.wait_recv()
        return wait

    tap = {0: W2, 1: W1, 2: W0}
    fz_lo, fz_hi = flag("gz", -1), flag("gz", 1)
    fy_lo, fy_hi = flag("gy", -1), flag("gy", 1)

    def own_sum(load, o, n, ghosts_hi, last):
        if not isinstance(o, int):
            c = 2 * o
            return W0 * (load(c - 2) + load(c + 2)) + W1 * (load(c - 1) + load(c + 1)) \
                + W2 * load(c)
        total = None
        for i in range(2 * o - 2, 2 * o + 3):
            if i < (-1 if ghosts_hi else 0) or i >= n + ghosts_hi:
                continue
            term = tap[abs(i - 2 * o)] * load(i if i >= 0 else last)
            total = term if total is None else total + term
        if o < 0:
            total = total * fz_lo
        elif o >= n // 2:
            total = total * fz_hi
        return total

    def row_sum(lev, s, lt):
        zz = z[lev]
        half = (zz.shape[2] - 32) // 2

        def load(k):
            return zz[s, lt, pl.ds(6 + k, half + 8, 2), :]
        x = W0 * (load(0) + load(4)) + W1 * (load(1) + load(3)) + W2 * load(2)
        lo = (W1 * zz[s, lt, 7:8, :] + W0 * zz[s, lt, 8:9, :]) * fy_lo
        row = lax.broadcasted_iota(jnp.int32, (8, LANES), 0)
        ghost = jnp.where(row < 2, x[half:half + 8] * fy_hi, jnp.where(row == 7, lo, 0.0))
        t[lev][lt, s, 0:half, :] = x[0:half]
        t[lev][lt, s, half:half + 8, :] = ghost

    def tile_of(tt, i):
        x = tt[i]
        return x.reshape(x.shape[0] * x.shape[1], LANES)

    def put(lev, j, x):
        out = sh[lev]
        out[:, j] = x.reshape(out.shape[0], out.shape[2], LANES)

    def columns(lev, tiles):
        tt = t[lev]
        parts = [split3(tile_of(tt, i)) for i in range(tt.shape[0])]
        for j in range(tiles // 2):
            ids = [2 * j - 1, 2 * j, 2 * j + 1, 2 * j + 2]
            lo, hi = 0, 4
            if j == 0:
                ids[0] = tiles
                lo = 1 if lev == 0 else 0
            if j == tiles // 2 - 1 and lev == 0:
                hi = 3
            put(lev, j, dots([parts[i] for i in ids[lo:hi]], wm[lo * LANES:hi * LANES]))
        if lev == 0:
            w = jnp.concatenate([wh[0:LANES], wh[2 * LANES:3 * LANES]], axis=0)
            out = dots([parts[tiles - 1], parts[0]], w)
        else:
            out = dots([parts[i] for i in (tiles - 1, tiles, 0)], wh[...])
        lane = lax.broadcasted_iota(jnp.int32, out.shape, 1)
        keep_hi = jnp.where(has["gx", 1], 1, 0)
        keep_lo = jnp.where(has["gx", -1], 1, 0)
        keep = jnp.where(lane < LANES // 2, keep_hi, keep_lo)
        put(lev, tiles // 2, jnp.where(keep > 0, out, 0.0))

    def send_shares(lev):
        s = sh[lev]
        n, rows = nz >> (lev + 1), s.shape[2] - 8
        g = s.shape[0] - n - 1
        ys_hi[lev][...] = s[:, :, rows:rows + g, :]
        ys_lo[lev][...] = s[:, :, rows + 7:rows + 8, :]
        ups, downs, sections = [], [], []
        for i, (d, snd, rcv, waits) in enumerate((
                (1, ys_hi[lev], yr_lo[lev], ups), (-1, ys_lo[lev], yr_hi[lev], downs))):
            for k, (steps, part) in enumerate((
                    ({"gy": d}, pl.ds(0, n)),
                    ({"gz": 1, "gy": d}, pl.ds(n, g)),
                    ({"gz": -1, "gy": d}, pl.ds(n + g, 1)))):
                at = 6 * lev + 3 * i + k
                waits.append(send(steps, snd.at[part], rcv.at[part], ysend.at[at], yrecv.at[at]))
        sections.append(send(
            {"gz": 1}, s.at[pl.ds(n, g), :, pl.ds(0, rows), :], rz_lo[lev],
            zsend.at[2 * lev], zrecv.at[2 * lev]))
        sections.append(send(
            {"gz": -1}, s.at[pl.ds(n + g, 1), :, pl.ds(0, rows), :], rz_hi[lev],
            zsend.at[2 * lev + 1], zrecv.at[2 * lev + 1]))
        return sections, ups + downs

    def take_sections(lev, tiles):
        s = sh[lev]
        n, rows = nz >> (lev + 1), s.shape[2] - 8
        g = s.shape[0] - n - 1

        @pl.when(has["gz", -1])
        def _():
            s[0:g, tiles, 0:rows, :] += rz_lo[lev][:, tiles]

        @pl.when(has["gz", 1])
        def _():
            s[n - 1:n, tiles, 0:rows, :] += rz_hi[lev][:, tiles]

    def take_rows(lev, tiles):
        s = sh[lev]
        n, rows = nz >> (lev + 1), s.shape[2] - 8
        g = s.shape[0] - n - 1
        for rcv, r, h in ((yr_lo[lev], 0, g), (yr_hi[lev], rows - 1, 1)):
            for i in range(n):
                add = rcv[i, tiles]
                if i < g:
                    add = add + rcv[n + i, tiles]
                if i == n - 1:
                    add = add + rcv[n + g, tiles]
                s[i, tiles, r:r + h, :] += add

    m = nz // 2

    def sections_first(o, at, r0, rn):
        for r in range(r0, r0 + rn, 8):
            for lt in range(nt):
                cols = slice(lt * LANES, (lt + 1) * LANES)
                z[0][at, lt, 8 + r:16 + r, :] = own_sum(
                    lambda i: v[i, r:r + 8, cols], o, nz, 0, 0)

    for c, (r0, rn) in zip(loads, groups):
        c.wait()

        @pl.loop(1, m - 1)
        def _(o):
            sections_first(o, o, r0, rn)
        for o, at in ((0, 0), (m - 1, m - 1), (m, m), (-1, m + 1)):
            sections_first(o, at, r0, rn)

    @pl.loop(0, m + 2)
    def _(o):
        for lt in range(nt):
            row_sum(0, o, lt)
    columns(0, nt)
    pl.semaphore_wait(barrier, sum(exists(p).astype(jnp.int32) for p in peers))
    waits = [send_shares(0)]

    for lev in (1, 2):
        src = sh[lev - 1]
        n = nz >> lev
        rows = src.shape[2] - 8
        g = src.shape[0] - n - 1
        tiles = src.shape[1] - 1
        outs = [(o, o) for o in range(n // 2 + 2)] + [(-1, n // 2 + 2)]
        for o, at in outs:
            for lt in range(tiles + 1):
                x = own_sum(lambda i: src[i, lt], o, n, g, n + g)
                z[lev][at, lt, 8:16 + rows, :] = x
                z[lev][at, lt, 0:8, :] = x[rows:rows + 8]
        for o, at in outs:
            for lt in range(tiles + 1):
                row_sum(lev, at, lt)
        columns(lev, tiles)
        waits.append(send_shares(lev))

    for lev in range(3):
        for w in waits[lev][0]:
            w()
        take_sections(lev, pl.ds(sh[lev].shape[1] - 1, 1))
    for lev in range(3):
        for w in waits[lev][1]:
            w()
        take_rows(lev, pl.ds(sh[lev].shape[1] - 1, 1))
    outs = (out1, out2, out3)
    flat = []
    for lev in range(3):
        n, rows, last = nz >> (lev + 1), sh[lev].shape[2] - 8, sh[lev].shape[1] - 1
        flat.append(sh[lev][0:n, last, 0:rows, :].reshape(n * rows, LANES))
    used = sum(f.shape[0] for f in flat)
    if xr.shape[1] > used:
        flat.append(jnp.zeros((xr.shape[1] - used, LANES), jnp.float32))
    packed = jnp.concatenate(flat, axis=0).T
    xs[0:8, :] = packed[0:8, :]
    xs[8:16, :] = packed[LANES - 8:LANES, :]
    columns_wait = [
        send({"gx": 1}, xs.at[pl.ds(0, 8)], xr.at[pl.ds(0, 8)], xsend.at[0], xrecv.at[0]),
        send({"gx": -1}, xs.at[pl.ds(8, 8)], xr.at[pl.ds(LANES - 8, 8)], xsend.at[1],
             xrecv.at[1])]

    for lev in range(3):
        take_sections(lev, pl.ds(0, sh[lev].shape[1] - 1))
        take_rows(lev, pl.ds(0, sh[lev].shape[1] - 1))

    def store(lev, j, x):
        outs[lev][:, :, j * LANES:(j + 1) * LANES] = x

    for lev in range(3):
        n, rows, count = nz >> (lev + 1), sh[lev].shape[2] - 8, sh[lev].shape[1] - 1
        for j in range(1, count - 1):
            store(lev, j, sh[lev][0:n, j, 0:rows, :])
    for w in columns_wait:
        w()
    back = xr[...].T
    start = 0
    for lev in range(3):
        n, rows, count = nz >> (lev + 1), sh[lev].shape[2] - 8, sh[lev].shape[1] - 1
        add = back[start:start + n * rows].reshape(n, rows, LANES)
        start += n * rows
        lane = lax.broadcasted_iota(jnp.int32, add.shape, 2)
        at_lo = jnp.where(lane < 2, add, 0.0)
        at_hi = jnp.where(lane == LANES - 1, add, 0.0)
        x = sh[lev][0:n, 0, 0:rows, :] + at_lo
        if count == 1:
            store(lev, 0, x + at_hi)
        else:
            store(lev, 0, x)
            store(lev, count - 1, sh[lev][0:n, count - 1, 0:rows, :] + at_hi)

    for steps, copy in sent:
        @pl.when(exists(steps))
        def _():
            copy.wait_send()


def write_out(a1, a2, a3, out1, out2, out3, sem):
    copies = [
        pltpu.make_async_copy(src, dst, sem.at[i])
        for i, (src, dst) in enumerate(((a1, out1), (a2, out2), (a3, out3)))]
    for c in copies:
        c.start()
    for c in copies:
        c.wait()


def on_device(sizes, volume):
    f32 = jnp.float32
    nz, ny, nx = volume.shape
    nt = nx // LANES
    V = pltpu.VMEM
    extra = (2, 3, 3)
    ins = (nt, (nt >> 1) + 1, (nt >> 2) + 1)
    n = [nz >> (l + 1) for l in range(3)]
    rows = [ny >> (l + 1) for l in range(3)]
    outs = [(nt >> (l + 1)) + 1 for l in range(3)]
    levels = range(3)
    z = [V((n[l] + extra[l], ins[l], 2 * rows[l] + 32, LANES), f32) for l in levels]
    t = [V((ins[l], n[l] + extra[l], rows[l] + 8, LANES), f32) for l in levels]
    sh = [V((n[l] + extra[l], outs[l], rows[l] + 8, LANES), f32) for l in levels]
    rz_lo = [V((extra[l] - 1, outs[l], rows[l], LANES), f32) for l in levels]
    rz_hi = [V((1, outs[l], rows[l], LANES), f32) for l in levels]
    lows = [V((n[l] + extra[l], outs[l], 1, LANES), f32) for l in levels]
    highs = [V((n[l] + extra[l], outs[l], extra[l] - 1, LANES), f32) for l in levels]
    packed = -(-sum(n[l] * rows[l] for l in levels) // LANES) * LANES
    dma = pltpu.SemaphoreType.DMA
    hbm = pl.BlockSpec(memory_space=pltpu.HBM)
    vmem = pl.BlockSpec(memory_space=pltpu.VMEM)
    volume = pltpu.with_memory_space_constraint(volume, pltpu.HBM)
    results = pl.pallas_call(
        functools.partial(kernel, sizes, (nz, ny, nt)),
        out_shape=tuple(
            V((nz >> l, ny >> l, nx >> l), f32) for l in (1, 2, 3)),
        in_specs=[hbm],
        out_specs=(vmem, vmem, vmem),
        scratch_shapes=[
            V((nz, ny, nx), f32), z, t, sh, rz_lo, rz_hi, lows, highs, highs, lows,
            V((16, packed), f32), V((LANES, packed), f32),
            V((4 * LANES, LANES), jnp.bfloat16), V((3 * LANES, LANES), jnp.bfloat16),
            dma((ny // 8,)),
            dma((6,)), dma((6,)), dma((18,)), dma((18,)), dma((2,)), dma((2,)),
        ],
        compiler_params=pltpu.CompilerParams(
            collective_id=0, has_side_effects=True, vmem_limit_bytes=40 << 20),
        name="pyramid",
    )(volume)
    return pl.pallas_call(
        write_out,
        out_shape=tuple(jax.ShapeDtypeStruct(x.shape, f32) for x in results),
        in_specs=[vmem] * 3,
        out_specs=(hbm, hbm, hbm),
        scratch_shapes=[dma((3,))],
        compiler_params=pltpu.CompilerParams(vmem_limit_bytes=4 << 20),
        name="write_out",
    )(*results)


def solution(mesh):
    sizes = {a: mesh.shape[a] for a in AXES}
    spec = P(*AXES)
    return jax.shard_map(
        functools.partial(on_device, sizes), mesh=mesh, in_specs=(spec,),
        out_specs=(spec, spec, spec), check_vma=False)
```

profile of v0, /device:TPU:0, one launch (start us, length us, event | category | flops | bytes accessed | tf_op | source)
XLA Modules:
  0.0 16.3 jit_solution(17175287999727390227)
XLA Ops:
  0.6 14.9 %pyramid.1 = (f32[8,32,512]{2,1,0:T(8,128)S(1)}, f32[4,16,256]{2,1,0:T(8,128)S(1)}, f32[2,8,128]{2,1,0:T(8,128)S(1)}) custom-call(f32[16,64,1024]{2,1,0:T(8,128)} %vol.1), custom_call_target="tpu_custom_call" | custom-call | tf_op jit(solution)/shard_map/pyramid/pallas_call | solution.py:383
  15.5 0.8 %write_out.1 = (f32[8,32,512]{2,1,0:T(8,128)}, f32[4,16,256]{2,1,0:T(8,128)}, f32[2,8,128]{2,1,0:T(8,128)}) custom-call(f32[8,32,512]{2,1,0:T(8,128)S(1)} %get-tuple-element.6.a1, f32[4,16,256]{2,1,0:T(8,128)S(1)} %get-tuple-element.7.a2, f32[2,8,128]{2,1,0:T(8,128)S(1)} %get-tuple-element.8.a3), custom_call_target="tpu_custom_call" | custom-call | tf_op jit(solution)/shard_map/write_out/pallas_call | solution.py:400
where the time goes:
time: 16.5 us; the launch traced here: 16.3 us
  Pallas kernels  15.7 us (95%)
  between operations  0.64 us (4%)
    pallas_call x1, Pallas kernels, on_device(): pl.pallas_call(functools.partial(kernel, sizes, (nz, ny, nt)), out_shape=...  14.9 us
    pallas_call x1, Pallas kernels, on_device(): pl.pallas_call(write_out, out_shape=tuple((jax.ShapeDtypeStruct(x.shape,...  0.83 us

commit v1 on v0

v1 whole, which is shorter than its diff:
```python
import functools
import itertools

import jax
import jax.numpy as jnp
import numpy as np
from jax import lax
from jax.experimental import pallas as pl
from jax.experimental.pallas import tpu as pltpu
from jax.sharding import PartitionSpec as P

LANES = 128
MESH = pl.DeviceIdType.MESH
AXES = ("gz", "gy", "gx")
TAPS = {-2: 1, -1: 4, 0: 6, 1: 4, 2: 1}
HI = (1, 2, 2)
WIDE = (256, 128, 128)
f32, bf16 = jnp.float32, jnp.bfloat16


def chain(n, lo, hi):
    prev = {i: {i: 1} for i in range(n)}
    levels = []
    for lev in range(3):
        n //= 2
        cur = {}
        for o in range(-1 if lo else 0, n + (HI[lev] if hi else 0)):
            col = {}
            for j, w in TAPS.items():
                for k, v in prev.get(2 * o + j, {}).items():
                    col[k] = col.get(k, 0) + w * v
            cur[o] = col
        levels.append(cur)
        prev = cur
    return levels


def split2(x):
    hi = x.astype(bf16)
    return hi, (x - hi.astype(f32)).astype(bf16)


def blocks_of(lev, nt):
    per = WIDE[lev] * (2 << lev) // LANES
    return [(b, list(range(max(per * b - 1, 0), min(per * (b + 1) + 1, nt))))
            for b in range(nt // per)]


class Rows:
    def __init__(self, m, tiles):
        self.own, at = [], 0
        for lev in range(3):
            self.own.append(at)
            at += HI[lev] * tiles[lev] * m[lev]
        self.n_own = -(-at // 8) * 8
        self.hi, at = [], self.n_own
        for lev in range(3):
            self.hi.append(at)
            at += HI[lev] * tiles[lev] * HI[lev]
        self.n_hi = -(-(at - self.n_own) // 8) * 8
        self.lo, at = [], self.n_own + self.n_hi
        for lev in range(3):
            self.lo.append(at)
            at += HI[lev] * tiles[lev]
        self.n_lo = -(-(at - self.n_own - self.n_hi) // 8) * 8
        self.total = self.n_own + self.n_hi + self.n_lo


def conv(load):
    return (load(-2) + load(2)) + 4.0 * (load(-1) + load(1)) + 6.0 * load(0)


def partial_conv(load, o, lo, hi):
    have = [j for j in TAPS if lo <= 2 * o + j < hi]
    if len(have) == 5:
        return conv(lambda j: load(2 * o + j))
    total = None
    for j in have:
        term = load(2 * o + j)
        if TAPS[j] != 1:
            term = float(TAPS[j]) * term
        total = term if total is None else total + term
    return total


def kernel(sizes, dims, vol, out1, out2, out3,
           v, Z, A2Z, A3Z, EA1, EA2, EG2, EG3, YG, YX, LX1, LX2, LX3,
           W1, W2, W3, WG, DS, YS, YR, XS, XR, ZS, ZR,
           load_sem, send_sem, recv_sem):
    nz, ny, nt = dims
    m = [nz >> 1, nz >> 2, nz >> 3]
    rw = [ny >> 1, ny >> 2, ny >> 3]
    ext = [m[l] + 1 + HI[l] for l in range(3)]
    tiles = [nt >> 1, nt >> 2, nt >> 3]
    ZP, P2, P3 = ny + 3, rw[0] + 3, rw[1] + 3
    E1P, E2P = 2 * ext[1] + 3, 2 * ext[2] + 3
    rowmap = Rows(m, tiles)
    outs = (out1, out2, out3)

    idx = {a: lax.axis_index(a) for a in AXES}
    has, near = {}, {}
    for a in AXES:
        has[a, -1], has[a, 1] = idx[a] > 0, idx[a] < sizes[a] - 1
        near[a, -1] = jnp.maximum(idx[a] - 1, 0)
        near[a, 1] = jnp.minimum(idx[a] + 1, sizes[a] - 1)

    def exists(steps):
        found = None
        for a, d in steps.items():
            found = has[a, d] if found is None else jnp.logical_and(found, has[a, d])
        return found

    def device(steps):
        return {a: near[a, d] for a, d in steps.items()}

    def flag(a, d):
        return jnp.where(has[a, d], 1.0, 0.0).astype(f32)

    fz_lo, fz_hi = flag("gz", -1), flag("gz", 1)
    fy_lo, fy_hi = flag("gy", -1), flag("gy", 1)
    fx_lo, fx_hi = flag("gx", -1), flag("gx", 1)

    low, high = 8, ny - 16
    loads = []
    for i, (r0, rn) in enumerate(((0, low), (high, 16), (low, high - low))):
        c = pltpu.make_async_copy(
            vol.at[:, pl.ds(r0, rn), :], v.at[:, pl.ds(r0, rn), :], load_sem.at[i])
        c.start()
        loads.append(c)

    YR[...] = jnp.zeros(YR.shape, f32)
    XR[...] = jnp.zeros(XR.shape, f32)
    ZR[...] = jnp.zeros(ZR.shape, f32)
    peers = []
    for dz, dy, dx in itertools.product((0, -1, 1), repeat=3):
        p = {a: d for a, d in zip(AXES, (dz, dy, dx)) if d}
        if p:
            peers.append(p)
    barrier = pltpu.get_barrier_semaphore()
    for p in peers:
        @pl.when(exists(p))
        def _():
            pl.semaphore_signal(barrier, inc=1, device_id=device(p), device_id_type=MESH)

    zero = jnp.zeros((8, LANES), f32)

    def clear(ref, at, n):
        ref[at:at + n] = jnp.zeros((n, LANES), f32)

    clear(Z, 0, 2)

    @pl.loop(1, nt * ext[0])
    def _(i):
        Z[pl.ds(i * ZP - 1, 3)] = jnp.zeros((3, LANES), f32)
    clear(Z, nt * ext[0] * ZP - 1, 1)
    for s in range(ext[1]):
        clear(A2Z, s * P2, 1)
    for s in range(ext[2]):
        clear(A3Z, s * P3, 1)
    EA1[...] = jnp.zeros(EA1.shape, f32)
    EA2[...] = jnp.zeros(EA2.shape, f32)
    YG[...] = jnp.zeros(YG.shape, f32)

    row8 = lax.broadcasted_iota(jnp.int32, (8, LANES), 0)
    lane = lax.broadcasted_iota(jnp.int32, (8, LANES), 1)
    nx = nt * LANES
    full, no_lo, no_hi = chain(nx, True, True), chain(nx, False, True), chain(nx, True, False)

    def spots(entries):
        x = jnp.zeros((8, LANES), f32)
        for r, c, val in entries:
            x = jnp.where(jnp.logical_and(row8 == r, lane == c), float(val), x)
        return x

    def fixes(lev, other):
        found = {}
        for c in range(nx >> (lev + 1)):
            for k, val in full[lev][c].items():
                gone = val - other[lev].get(c, {}).get(k, 0)
                if gone:
                    found[k, c] = gone
        return found

    for lev, W in ((0, W1), (1, W2), (2, W3)):
        step = 2 << lev
        mid = (nx >> (lev + 1)) // 2
        tap = {k - step * mid: w for k, w in full[lev][mid].items()}
        reach = max(tap)
        scale = 2.0 ** (-12 * (lev + 1))
        signed = jnp.where(lane < LANES // 2, lane, lane - LANES)
        delta = row8 - step * signed
        dist = jnp.abs(delta)
        base = jnp.zeros((8, LANES), f32)
        for d in range(reach + 1):
            base = jnp.where(dist == d, tap[d] * scale, base)
        lo_fix, hi_fix = fixes(lev, no_lo), fixes(lev, no_hi)
        for b, lts in blocks_of(lev, nt):
            for part in range(WIDE[lev] // LANES):
                c0 = WIDE[lev] * b + LANES * part
                for kk in range(0, len(lts) * LANES, 16):
                    pieces = []
                    for k8 in (kk, kk + 8):
                        k = lts[0] * LANES + k8
                        first = -((-(k - reach)) // step) - c0
                        last = (k + 7 + reach) // step - c0
                        if last < 0 or first >= LANES:
                            pieces.append(zero)
                            continue
                        x = pltpu.roll(base, (k // step - c0) % LANES, 1)
                        if first < 0:
                            x = jnp.where(lane <= last, x, 0.0)
                        elif last >= LANES:
                            x = jnp.where(lane >= first, x, 0.0)
                        for fix, fl in ((lo_fix, fx_lo), (hi_fix, fx_hi)):
                            here = [(r - k, c - c0, val * scale) for (r, c), val in fix.items()
                                    if k <= r < k + 8 and c0 <= c < c0 + LANES]
                            if here:
                                x = x - (1.0 - fl) * spots(here)
                        pieces.append(x)
                    w = jnp.concatenate(pieces, axis=0)
                    hi = w.astype(bf16)
                    cols = slice(part * LANES, (part + 1) * LANES)
                    if lev < 2:
                        W[b, kk:kk + 16, cols] = hi
                    else:
                        W[b, kk:kk + 16, 0:LANES] = hi
                        W[b, kk:kk + 16, LANES:2 * LANES] = (w - hi.astype(f32)).astype(bf16)

    for lev in range(3):
        n = nx >> (lev + 1)
        scale = 2.0 ** (-12 * (lev + 1))
        entries = []
        for r, c in [(0, n), (7, -1)] + ([(1, n + 1)] if HI[lev] == 2 else []):
            for k, val in full[lev][c].items():
                entries.append((r, k if k < LANES // 2 else k - nx + LANES, val * scale))
        x = spots(entries)
        hi, lo = split2(x)
        both = jnp.concatenate([hi.astype(f32), lo.astype(f32)], axis=0)
        WG[16 * lev:16 * lev + 16] = both.astype(bf16)

    def z_block(lt, r, base):
        cols = pl.ds(pl.multiple_of(lt * LANES, LANES), LANES)
        x = [v[i, r:r + 8, cols] for i in range(nz)]
        for s in range(ext[0]):
            o = s - 1
            y = partial_conv(lambda i: x[i], o, 0, nz)
            if o < 0:
                y = y * fz_lo
            elif o >= m[0]:
                y = y * fz_hi
            Z[pl.ds(base + s * ZP + r + 2, 8)] = y

    def zrow(n, mz):
        row = lax.broadcasted_iota(jnp.int32, (n, LANES), 0)
        return jnp.where(row == 0, fz_lo, jnp.where(row > mz, fz_hi, 1.0))

    def edge(lt, base):
        src = {}

        def zy(y):
            if y not in src:
                src[y] = Z[pl.ds(base + y + 2, ext[0], ZP)]
            return src[y]
        f2, f3 = zrow(ext[1], m[1]), zrow(ext[2], m[2])
        n1, n2, n3 = rw
        rows1 = [-1, 0, 1, 2] + list(range(n1 - 6, n1 + 1))
        a2z = {}
        for k, e in enumerate(rows1):
            x = partial_conv(zy, e, 0, ny)
            EA1[k * E1P + 3:k * E1P + 3 + ext[0]] = x
            if e == -1:
                YG[0:ext[0]] = x
            elif e == n1:
                YG[16:16 + ext[0]] = x
        for k, e in enumerate(rows1):
            a2z[e] = conv(lambda j: EA1[pl.ds(k * E1P + 2 + j, ext[1], 2)]) * f2
        at = pl.multiple_of(lt * 16, 8)
        EG2[pl.ds(at, ext[1])] = a2z[-1]
        EG2[pl.ds(at + 8, ext[1])] = a2z[n1]
        rows2 = [-1, 0, n2 - 2, n2 - 1, n2, n2 + 1]
        a3z = {}
        for k, e in enumerate(rows2):
            x = partial_conv(lambda i: a2z[i], e, -1, n1 + 1)
            EA2[k * E2P + 3:k * E2P + 3 + ext[1]] = x
            if e in (-1, n2, n2 + 1):
                r = 32 + 8 * (0, n2, n2 + 1).index(max(e, 0))
                YG[r:r + ext[1]] = x
        for k, e in enumerate(rows2):
            a3z[e] = conv(lambda j: EA2[pl.ds(k * E2P + 2 + j, ext[2], 2)]) * f3
        EG3[pl.ds(at, ext[2])] = a3z[-1]
        EG3[pl.ds(at + 8, ext[2])] = a3z[n2]
        for k, e in enumerate((-1, n3, n3 + 1)):
            x = partial_conv(lambda i: a3z[i], e, -1, n2 + 2)
            YG[64 + 8 * k:64 + 8 * k + ext[2]] = x
        cols = pl.ds(pl.multiple_of(lt * LANES, LANES), LANES)
        for lev in range(3):
            hi, mid = split2(YG[32 * lev:32 * lev + 32])
            YX[64 * lev:64 * lev + 32, cols] = hi
            YX[64 * lev + 32:64 * lev + 64, cols] = mid

    order3 = list(range(1, ext[2])) + [0]

    def main(lt, base):
        cols = pl.ds(pl.multiple_of(lt * LANES, LANES), LANES)
        at = pl.multiple_of(lt * 16, 8)
        A2Z[pl.ds(1, ext[1], P2)] = EG2[pl.ds(at, ext[1])] * fy_lo
        A2Z[pl.ds(rw[0] + 2, ext[1], P2)] = EG2[pl.ds(at + 8, ext[1])] * fy_hi
        A3Z[pl.ds(1, ext[2], P3)] = EG3[pl.ds(at, ext[2])] * fy_lo
        A3Z[pl.ds(rw[1] + 2, ext[2], P3)] = EG3[pl.ds(at + 8, ext[2])] * fy_hi

        def reduce_sections(x, lev):
            for s in range(ext[lev]):
                y = partial_conv(lambda i: x[i + 1], s - 1, -1, len(x) - 1)
                if s == 0:
                    y = y * fz_lo
                elif s > m[lev]:
                    y = y * fz_hi
                yield s, y

        for q in range(0, rw[0], 16):
            x = []
            for s in range(ext[0]):
                half = [conv(lambda j: Z[pl.ds(base + s * ZP + 2 * (q + h) + 2 + j, 8, 2)])
                        for h in (0, 8)]
                y = jnp.concatenate(half, axis=0)
                hi, mid = split2(y)
                r = s * rw[0] + q
                LX1[r:r + 16, cols] = hi
                LX1[ext[0] * rw[0] + r:ext[0] * rw[0] + r + 16, cols] = mid
                x.append(y)
            for s, y in reduce_sections(x, 1):
                A2Z[s * P2 + q + 2:s * P2 + q + 18] = y
        for q in range(0, rw[1], 16):
            x = []
            for s in range(ext[1]):
                half = [conv(lambda j: A2Z[pl.ds(s * P2 + 2 * (q + h) + 2 + j, 8, 2)])
                        for h in (0, 8)]
                y = jnp.concatenate(half, axis=0)
                hi, mid = split2(y)
                r = s * rw[1] + q
                LX2[r:r + 16, cols] = hi
                LX2[ext[1] * rw[1] + r:ext[1] * rw[1] + r + 16, cols] = mid
                x.append(y)
            for s, y in reduce_sections(x, 2):
                A3Z[s * P3 + q + 2:s * P3 + q + 18] = y
        x = {}
        for s in range(ext[2]):
            x[s] = conv(lambda j: A3Z[pl.ds(s * P3 + 2 + j, 8, 2)])
        n = LX3.shape[0] // 2
        for i in range(0, n // 8, 2):
            pair = [x[order3[k]] if k < ext[2] else zero for k in (i, i + 1)]
            hi, mid = split2(jnp.concatenate(pair, axis=0))
            LX3[8 * i:8 * i + 16, cols] = hi
            LX3[n + 8 * i:n + 8 * i + 16, cols] = mid

    def columns(lev, rows_of):
        W = (W1, W2, W3)[lev]
        for b, lts in blocks_of(lev, nt):
            x = rows_of(slice(lts[0] * LANES, (lts[-1] + 1) * LANES))
            d = jnp.dot(x, W[b, 0:len(lts) * LANES], preferred_element_type=f32)
            n = x.shape[0] // 2
            d = d[0:n] + d[n:2 * n]
            if lev == 2:
                yield b, d[:, 0:LANES] + d[:, LANES:2 * LANES]
            else:
                for part in range(WIDE[lev] // LANES):
                    yield (b * (WIDE[lev] // LANES) + part,
                           d[:, part * LANES:(part + 1) * LANES])

    lane_k = lax.broadcasted_iota(jnp.int32, (16, LANES), 1) < LANES // 2

    def ends(ref, r, n):
        pieces = []
        for i in range(r, r + n, 16):
            a = ref[i:i + 16, 0:LANES].astype(f32)
            c = ref[i:i + 16, (nt - 1) * LANES:nt * LANES].astype(f32)
            pieces.append(jnp.where(lane_k, a, c).astype(bf16))
        return pieces

    def spill_columns(parts):
        his, mids = [], []
        for tile in parts:
            used = 0
            for lev, ref, r, n, off in tile:
                his += ends(ref, r, n)
                mids += ends(ref, r + off, n)
                used += n
            if used < LANES:
                fill = jnp.zeros((LANES - used, LANES), bf16)
                his.append(fill)
                mids.append(fill)
        rhs = jnp.concatenate(
            [jnp.concatenate(his, axis=0), jnp.concatenate(mids, axis=0)], axis=1)
        w = WG[...]
        lhs = jnp.concatenate([w, w], axis=1)
        d = lax.dot_general(lhs, rhs, (((1,), (1,)), ((), ())), preferred_element_type=f32)
        for i, tile in enumerate(parts):
            out, start = None, 0
            for lev, ref, r, n, off in tile:
                cols = slice(i * LANES, (i + 1) * LANES)
                x = d[16 * lev:16 * lev + 8, cols] + d[16 * lev + 8:16 * lev + 16, cols]
                out = x if out is None else jnp.where(lane >= start, x, out)
                start += n
            yield out

    sent = []

    def send(steps, src, dst):
        at = len(sent)
        copy = pltpu.make_async_remote_copy(
            src_ref=src, dst_ref=dst, send_sem=send_sem.at[at], recv_sem=recv_sem.at[at],
            device_id=device(steps), device_id_type=MESH)

        @pl.when(exists(steps))
        def _():
            copy.start()
        sent.append((steps, copy))

    for c in loads[0:2]:
        c.wait()

    @pl.loop(0, nt)
    def _(lt):
        base = lt * (ext[0] * ZP)
        for r in [0] + list(range(high, ny, 8)):
            z_block(lt, r, base)
        edge(lt, base)

    for lev in range(3):
        for t, d in columns(lev, lambda cols: YX[64 * lev:64 * lev + 64, cols]):
            DS[32 * t:32 * t + 32] = d
            e, mm, h = 16 if lev == 0 else 8, m[lev], HI[lev]
            for side in (0, 1):
                for k in range(h if side else 1):
                    r = 32 * t + e * (side + k)
                    slot = k * tiles[lev] + t
                    to = rowmap.own[lev] + slot * mm
                    YS[side, to:to + mm] = DS[r + 1:r + 1 + mm]
                    to = rowmap.hi[lev] + slot * h
                    YS[side, to:to + h] = DS[r + 1 + mm:r + 1 + mm + h]
                    to = rowmap.lo[lev] + slot
                    YS[side, to:to + 1] = DS[r:r + 1]
    spill = spill_columns([[(lev, YX, 64 * lev, 32, 32) for lev in range(3)]])
    XS[5] = next(spill)

    pl.semaphore_wait(barrier, sum(exists(p).astype(jnp.int32) for p in peers))
    segments = ((0, 0, rowmap.n_own), (1, rowmap.n_own, rowmap.n_hi),
                (-1, rowmap.n_own + rowmap.n_hi, rowmap.n_lo))

    def steps_of(dx, dy, dz):
        return {a: d for a, d in (("gz", dz), ("gy", dy), ("gx", dx)) if d}

    for dx in (1, -1):
        for dy in (1, -1):
            for dz in (0, 1, -1):
                slot = 5 + 3 * (dy < 0) + (0, 1, -1).index(dz)
                send(steps_of(dx, dy, dz), XS.at[5], XR.at[int(dx < 0), slot])
    for dy in (1, -1):
        side = int(dy > 0)
        for dz, at, n in segments:
            send(steps_of(0, dy, dz), YS.at[side, pl.ds(at, n)],
                 YR.at[int(dy < 0), pl.ds(at, n)])

    loads[2].wait()

    def tile_main(lt):
        base = lt * (ext[0] * ZP)
        for r in range(low, high, 8):
            z_block(lt, r, base)
        main(lt, base)

    @pl.loop(0, 2)
    def _(i):
        tile_main(i * (nt - 1))

    o1, o2 = ext[0] * rw[0], ext[1] * rw[1]
    o3 = LX3.shape[0] // 2
    own = [(0, LX1, rw[0] * (1 + i), LANES, o1) for i in range(0, m[0], LANES // rw[0])]
    parts = [[p] for p in own]
    parts.append([(1, LX2, rw[1], m[1] * rw[1], o2), (2, LX3, 0, m[2] * rw[2], o3)])
    parts.append([(0, LX1, rw[0] * (1 + m[0]), rw[0], o1),
                  (1, LX2, rw[1] * (1 + m[1]), 2 * rw[1], o2), (2, LX3, 16, 16, o3)])
    parts.append([(0, LX1, 0, rw[0], o1), (1, LX2, 0, rw[1], o2), (2, LX3, 32, 16, o3)])
    for i, x in enumerate(spill_columns(parts)):
        XS[i] = x
    for dx in (1, -1):
        side = int(dx < 0)
        send(steps_of(dx, 0, 0), XS.at[pl.ds(0, 3)], XR.at[side, pl.ds(0, 3)])
        send(steps_of(dx, 0, 1), XS.at[3], XR.at[side, 3])
        send(steps_of(dx, 0, -1), XS.at[4], XR.at[side, 4])

    @pl.loop(1, nt - 1)
    def _(lt):
        tile_main(lt)

    zat = [[0, 0, 0], [0, 0, 0]]
    at = [0, 0]
    for lev in range(3):
        for side in (0, 1):
            zat[side][lev] = at[side]
            at[side] += (HI[lev] if side else 1) * tiles[lev] * rw[lev]
    for lev, LX in ((0, LX1), (1, LX2), (2, LX3)):
        n, r = rw[lev], tiles[lev]
        for t, d in columns(lev, lambda cols: LX[:, cols]):
            for s in range(ext[lev]):
                i = order3.index(s) if lev == 2 else s
                x = d[i * n:(i + 1) * n]
                if s == 0:
                    to = zat[0][lev] + t * n
                    ZS[0, to:to + n] = x
                elif s > m[lev]:
                    to = zat[1][lev] + ((s - 1 - m[lev]) * r + t) * n
                    ZS[1, to:to + n] = x
                else:
                    to = ((s - 1) * r + t) * n
                    outs[lev][to:to + n] = x
    for dz in (1, -1):
        side = int(dz > 0)
        send(steps_of(0, 0, dz), ZS.at[side], ZR.at[side])

    def wait_all(which):
        for steps, copy in sent:
            if which(steps):
                @pl.when(exists({a: -d for a, d in steps.items()}))
                def _():
                    copy.wait_recv()

    wait_all(lambda s: "gx" not in s and "gy" in s)
    for lev in range(3):
        o, n, r, mm = outs[lev], rw[lev], tiles[lev], m[lev]
        pitch = r * n
        for side in (0, 1):
            for k in range(1 if side else HI[lev]):
                y = n - 1 if side else k
                for t in range(r):
                    slot = k * r + t
                    at = rowmap.own[lev] + slot * mm
                    x = YR[side, at:at + mm]
                    h = HI[lev]
                    at = rowmap.hi[lev] + slot * h
                    up = YR[side, at:at + h]
                    at = rowmap.lo[lev] + slot
                    down = YR[side, at:at + 1]
                    here = pl.ds(t * n + y, mm, pitch)
                    o[here] = o[here] + x
                    here = pl.ds(t * n + y, h, pitch) if h > 1 else pl.ds(t * n + y, 1)
                    o[here] = o[here] + up
                    here = pl.ds((mm - 1) * pitch + t * n + y, 1)
                    o[here] = o[here] + down

    wait_all(lambda s: "gx" in s and "gy" not in s)

    def unpack(lo, hi):
        x = jnp.concatenate([lo, jnp.zeros((LANES - 16, LANES), f32), hi], axis=0)
        return x.T

    def add_columns(lev, here, x):
        o = outs[lev]
        lanes = lax.broadcasted_iota(jnp.int32, x.shape, 1)
        a, c = jnp.where(lanes < 2, x, 0.0), jnp.where(lanes == LANES - 1, x, 0.0)
        for t, add in ((0, a), (tiles[lev] - 1, c)):
            if tiles[lev] == 1:
                if t == 0 and add is a:
                    o[here(0)] = o[here(0)] + (a + c)
                return
            o[here(t)] = o[here(t)] + add

    def section(lev, z, x):
        n = rw[lev]
        add_columns(lev, lambda t: pl.ds((z * tiles[lev] + t) * n, n), x)

    for i in range(len(own)):
        x = unpack(XR[0, i], XR[1, i])
        for j in range(LANES // rw[0]):
            section(0, i * (LANES // rw[0]) + j, x[j * rw[0]:(j + 1) * rw[0]])
    x = unpack(XR[0, 2], XR[1, 2])
    for z in range(m[1]):
        section(1, z, x[z * rw[1]:(z + 1) * rw[1]])
    at = m[1] * rw[1]
    for z in range(m[2]):
        section(2, z, x[at + z * rw[2]:at + (z + 1) * rw[2]])
    x = unpack(XR[0, 3], XR[1, 3])
    at = 0
    for lev in range(3):
        for z in range(HI[lev]):
            section(lev, z, x[at:at + rw[lev]])
            at += rw[lev]
    x = unpack(XR[0, 4], XR[1, 4])
    at = 0
    for lev in range(3):
        section(lev, m[lev] - 1, x[at:at + rw[lev]])
        at += rw[lev]

    wait_all(lambda s: "gx" in s and "gy" in s)
    lane96 = lane % 32
    kind_s = jnp.where(lane < 32, lane % 16, lane % 8)
    is_up = lane96 >= jnp.where(lane < 32, 16, 8)
    top = jnp.where(lane < 32, m[0], jnp.where(lane < 64, m[1], m[2]))

    def merge(side):
        total = jnp.zeros((8, LANES), f32)
        for j, up in ((0, True), (1, False)):
            for i in range(3):
                x = XR[side, 5 + 3 * j + i]
                if i == 0:
                    ok = jnp.logical_and(kind_s >= 1, kind_s <= top)
                elif i == 1:
                    ok = kind_s > top
                else:
                    ok = kind_s == 0
                ok = jnp.logical_and(ok, is_up if up else lane96 < jnp.where(lane < 32, 16, 8))
                total = jnp.where(ok, x, total)
        return total

    x = unpack(merge(0), merge(1))
    DS[0:LANES] = x
    for lev in range(3):
        n, r, mm, h = rw[lev], tiles[lev], m[lev], HI[lev]
        pitch = r * n
        e = 16 if lev == 0 else 8
        for side in (0, 1):
            for k in range(h if side else 1):
                at = 32 * lev + e * (side + k)
                y = k if side else n - 1
                add_columns(lev, lambda t: pl.ds(t * n + y, mm, pitch), DS[at + 1:at + 1 + mm])
                add_columns(
                    lev, lambda t: pl.ds(t * n + y, h, pitch) if h > 1 else pl.ds(t * n + y, 1),
                    DS[at + 1 + mm:at + 1 + mm + h])
                add_columns(lev, lambda t: pl.ds((mm - 1) * pitch + t * n + y, 1), DS[at:at + 1])

    wait_all(lambda s: "gx" not in s and "gy" not in s)
    for lev in range(3):
        o, n, r = outs[lev], rw[lev], tiles[lev]
        cnt = HI[lev] * r * n
        o[0:cnt] = o[0:cnt] + ZR[1, zat[1][lev]:zat[1][lev] + cnt]
        cnt, start = r * n, (m[lev] - 1) * r * n
        o[start:start + cnt] = o[start:start + cnt] + ZR[0, zat[0][lev]:zat[0][lev] + cnt]

    for steps, copy in sent:
        @pl.when(exists(steps))
        def _():
            copy.wait_send()


def write_out(a1, a2, a3, out1, out2, out3, sem):
    copies = []
    for src, dst in ((a1, out1), (a2, out2), (a3, out3)):
        for t in range(src.shape[1]):
            copies.append(pltpu.make_async_copy(
                src.at[:, t], dst.at[:, :, pl.ds(t * LANES, LANES)], sem.at[len(copies)]))
    for c in copies:
        c.start()
    for c in copies:
        c.wait()


def on_device(sizes, volume):
    nz, ny, nx = volume.shape
    nt = nx // LANES
    V = pltpu.VMEM
    m = [nz >> (l + 1) for l in range(3)]
    rw = [ny >> (l + 1) for l in range(3)]
    tiles = [nt >> (l + 1) for l in range(3)]
    ext = [m[l] + 1 + HI[l] for l in range(3)]
    ZP, P2, P3 = ny + 3, rw[0] + 3, rw[1] + 3
    E1P, E2P = 2 * ext[1] + 3, 2 * ext[2] + 3
    rowmap = Rows(m, tiles)
    n3 = -(-ext[2] * rw[2] // 16) * 16
    zrows = sum(HI[l] * tiles[l] * rw[l] for l in range(3))
    dma = pltpu.SemaphoreType.DMA
    hbm = pl.BlockSpec(memory_space=pltpu.HBM)
    vmem = pl.BlockSpec(memory_space=pltpu.VMEM)

    def flat(n):
        return V((-(-n // 8) * 8, LANES), f32)

    def weights(lev):
        found = blocks_of(lev, nt)
        depth = max(len(lts) for b, lts in found) * LANES
        return V((len(found), depth, 256 if lev == 2 else WIDE[lev]), bf16)

    volume = pltpu.with_memory_space_constraint(volume, pltpu.HBM)
    results = pl.pallas_call(
        functools.partial(kernel, sizes, (nz, ny, nt)),
        out_shape=tuple(V((m[l] * tiles[l] * rw[l], LANES), f32) for l in range(3)),
        in_specs=[hbm],
        out_specs=(vmem, vmem, vmem),
        scratch_shapes=[
            V((nz, ny, nx), f32),
            flat(nt * ext[0] * ZP), flat(ext[1] * P2), flat(ext[2] * P3),
            flat(11 * E1P), flat(6 * E2P), flat(16 * nt), flat(16 * nt), flat(96),
            V((192, nx), bf16),
            V((2 * ext[0] * rw[0], nx), bf16), V((2 * ext[1] * rw[1], nx), bf16),
            V((2 * n3, nx), bf16),
            weights(0), weights(1), weights(2), V((48, LANES), bf16),
            flat(LANES), V((2, rowmap.total, LANES), f32), V((2, rowmap.total, LANES), f32),
            V((6, 8, LANES), f32), V((2, 11, 8, LANES), f32),
            V((2, zrows, LANES), f32), V((2, zrows, LANES), f32),
            dma((3,)), dma((26,)), dma((26,)),
        ],
        compiler_params=pltpu.CompilerParams(
            collective_id=0, has_side_effects=True, vmem_limit_bytes=40 << 20),
        name="pyramid",
    )(volume)
    results = [x.reshape(m[l], tiles[l], rw[l], LANES) for l, x in enumerate(results)]
    return pl.pallas_call(
        write_out,
        out_shape=tuple(
            jax.ShapeDtypeStruct((nz >> l, ny >> l, nx >> l), f32) for l in (1, 2, 3)),
        in_specs=[vmem] * 3,
        out_specs=(hbm, hbm, hbm),
        scratch_shapes=[dma((sum(tiles),))],
        compiler_params=pltpu.CompilerParams(vmem_limit_bytes=4 << 20),
        name="write_out",
    )(*results)


def solution(mesh):
    sizes = {a: mesh.shape[a] for a in AXES}
    spec = P(*AXES)
    return jax.shard_map(
        functools.partial(on_device, sizes), mesh=mesh, in_specs=(spec,),
        out_specs=(spec, spec, spec), check_vma=False)
```

time: 16.5 us -> 10.9 us (0.66)
  Pallas kernels: 15.7 us -> 10.1 us
    pallas_call x1, Pallas kernels: 14.9 us -> 9.26 us  [on_device(): pl.pallas_call(functools.partial(kernel, sizes, (nz, ny, nt)), out_shape=...]
where the time goes in v1:
time: 10.9 us; the launch traced here: 10.8 us
  Pallas kernels  10.1 us (93%)
  between operations  0.64 us (6%)
    pallas_call x1, Pallas kernels, on_device(): pl.pallas_call(functools.partial(kernel, sizes, (nz, ny, nt)), out_shape=...  9.26 us
    pallas_call x1, Pallas kernels, on_device(): pl.pallas_call(write_out, out_shape=tuple((jax.ShapeDtypeStruct((nz >> l,...  0.86 us

profile of v1, /device:TPU:0, one launch (start us, length us, event | category | flops | bytes accessed | tf_op | source)
XLA Modules:
  0.0 10.8 jit_solution(14112764532442299356)
XLA Ops:
  0.6 9.3 %pyramid.1 = (f32[1024,128]{1,0:T(8,128)S(1)}, f32[128,128]{1,0:T(8,128)S(1)}, f32[16,128]{1,0:T(8,128)S(1)}) custom-call(f32[16,64,1024]{2,1,0:T(8,128)} %vol.1), custom_call_target="tpu_custom_call" | custom-call | tf_op jit(solution)/shard_map/pyramid/pallas_call | solution.py:683
  9.9 0.9 %write_out.1 = (f32[8,32,512]{2,1,0:T(8,128)}, f32[4,16,256]{2,1,0:T(8,128)}, f32[2,8,128]{2,1,0:T(8,128)}) custom-call(f32[8,4,32,128]{3,2,1,0:T(8,128)S(1)} %bitcast.3, f32[4,2,16,128]{3,2,1,0:T(8,128)S(1)} %bitcast.4, f32[2,1,8,128]{3,2,1,0:T(8,128)S(1)} %bitcast.5), custom_call_target="tpu_custom_call" | custom-call | tf_op jit(solution)/shard_map/write_out/pallas_call | solution.py:706

commit v2 on v1

--- a/solution.py
+++ b/solution.py
@@ -120,6 +120,13 @@
     fy_lo, fy_hi = flag("gy", -1), flag("gy", 1)
     fx_lo, fx_hi = flag("gx", -1), flag("gx", 1)
 
+    peers = []
+    for dx, dy, dz in itertools.product((-1, 1, 0), (-1, 1, 0), (1, -1, 0)):
+        p = {a: d for a, d in (("gz", dz), ("gy", dy), ("gx", dx)) if d}
+        if p:
+            peers.append(p)
+    barrier = pltpu.get_barrier_semaphore()
+
     low, high = 8, ny - 16
     loads = []
     for i, (r0, rn) in enumerate(((0, low), (high, 16), (low, high - low))):
@@ -127,20 +134,70 @@
             vol.at[:, pl.ds(r0, rn), :], v.at[:, pl.ds(r0, rn), :], load_sem.at[i])
         c.start()
         loads.append(c)
-
-    YR[...] = jnp.zeros(YR.shape, f32)
-    XR[...] = jnp.zeros(XR.shape, f32)
-    ZR[...] = jnp.zeros(ZR.shape, f32)
-    peers = []
-    for dz, dy, dx in itertools.product((0, -1, 1), repeat=3):
-        p = {a: d for a, d in zip(AXES, (dz, dy, dx)) if d}
-        if p:
-            peers.append(p)
-    barrier = pltpu.get_barrier_semaphore()
     for p in peers:
         @pl.when(exists(p))
         def _():
             pl.semaphore_signal(barrier, inc=1, device_id=device(p), device_id_type=MESH)
+
+    segments = ((0, 0, rowmap.n_own), (1, rowmap.n_own, rowmap.n_hi),
+                (-1, rowmap.n_own + rowmap.n_hi, rowmap.n_lo))
+    sent = []
+
+    def message(steps, src, dst):
+        at = len(sent)
+        sent.append((steps, dst, pltpu.make_async_remote_copy(
+            src_ref=src, dst_ref=dst, send_sem=send_sem.at[at], recv_sem=recv_sem.at[at],
+            device_id=device(steps), device_id_type=MESH)))
+
+    def steps_of(dx, dy, dz):
+        return {a: d for a, d in (("gz", dz), ("gy", dy), ("gx", dx)) if d}
+
+    for dx in (-1, 1):
+        for dy in (-1, 1):
+            for dz in (0, 1, -1):
+                slot = 5 + 3 * (dy < 0) + (0, 1, -1).index(dz)
+                message(steps_of(dx, dy, dz), XS.at[5], XR.at[int(dx < 0), slot])
+    for dy in (-1, 1):
+        for dz, at, n in segments:
+            message(steps_of(0, dy, dz), YS.at[int(dy > 0), pl.ds(at, n)],
+                    YR.at[int(dy < 0), pl.ds(at, n)])
+    for dx in (-1, 1):
+        side = int(dx < 0)
+        message(steps_of(dx, 0, 0), XS.at[pl.ds(0, 3)], XR.at[side, pl.ds(0, 3)])
+        message(steps_of(dx, 0, 1), XS.at[3], XR.at[side, 3])
+        message(steps_of(dx, 0, -1), XS.at[4], XR.at[side, 4])
+    for dz in (1, -1):
+        side = int(dz > 0)
+        message(steps_of(0, 0, dz), ZS.at[side], ZR.at[side])
+
+    def start(which, when=None):
+        for steps, dst, copy in sent:
+            if which(steps):
+                ok = exists(steps)
+
+                @pl.when(ok if when is None else jnp.logical_and(ok, when))
+                def _():
+                    copy.start()
+
+    for steps, dst, copy in sent:
+        @pl.when(jnp.logical_not(exists({a: -d for a, d in steps.items()})))
+        def _():
+            dst[...] = jnp.zeros(dst.shape, f32)
+
+    def with_rows(steps):
+        return "gy" in steps
+
+    def with_columns(steps):
+        return "gx" in steps and "gy" not in steps
+
+    def with_sections(steps):
+        return "gx" not in steps and "gy" not in steps
+
+    def meet():
+        pl.semaphore_wait(barrier, sum(exists(p).astype(jnp.int32) for p in peers))
+
+    first_tile = jnp.logical_not(jnp.logical_or(has["gx", -1], has["gy", -1]))
+    later_tile = jnp.logical_or(has["gx", -1], has["gy", -1])
 
     zero = jnp.zeros((8, LANES), f32)
 
@@ -403,19 +460,6 @@
                 start += n
             yield out
 
-    sent = []
-
-    def send(steps, src, dst):
-        at = len(sent)
-        copy = pltpu.make_async_remote_copy(
-            src_ref=src, dst_ref=dst, send_sem=send_sem.at[at], recv_sem=recv_sem.at[at],
-            device_id=device(steps), device_id_type=MESH)
-
-        @pl.when(exists(steps))
-        def _():
-            copy.start()
-        sent.append((steps, copy))
-
     for c in loads[0:2]:
         c.wait()
 
@@ -443,23 +487,10 @@
     spill = spill_columns([[(lev, YX, 64 * lev, 32, 32) for lev in range(3)]])
     XS[5] = next(spill)
 
-    pl.semaphore_wait(barrier, sum(exists(p).astype(jnp.int32) for p in peers))
-    segments = ((0, 0, rowmap.n_own), (1, rowmap.n_own, rowmap.n_hi),
-                (-1, rowmap.n_own + rowmap.n_hi, rowmap.n_lo))
-
-    def steps_of(dx, dy, dz):
-        return {a: d for a, d in (("gz", dz), ("gy", dy), ("gx", dx)) if d}
-
-    for dx in (1, -1):
-        for dy in (1, -1):
-            for dz in (0, 1, -1):
-                slot = 5 + 3 * (dy < 0) + (0, 1, -1).index(dz)
-                send(steps_of(dx, dy, dz), XS.at[5], XR.at[int(dx < 0), slot])
-    for dy in (1, -1):
-        side = int(dy > 0)
-        for dz, at, n in segments:
-            send(steps_of(0, dy, dz), YS.at[side, pl.ds(at, n)],
-                 YR.at[int(dy < 0), pl.ds(at, n)])
+    @pl.when(later_tile)
+    def _():
+        meet()
+        start(with_rows)
 
     loads[2].wait()
 
@@ -483,15 +514,17 @@
     parts.append([(0, LX1, 0, rw[0], o1), (1, LX2, 0, rw[1], o2), (2, LX3, 32, 16, o3)])
     for i, x in enumerate(spill_columns(parts)):
         XS[i] = x
-    for dx in (1, -1):
-        side = int(dx < 0)
-        send(steps_of(dx, 0, 0), XS.at[pl.ds(0, 3)], XR.at[side, pl.ds(0, 3)])
-        send(steps_of(dx, 0, 1), XS.at[3], XR.at[side, 3])
-        send(steps_of(dx, 0, -1), XS.at[4], XR.at[side, 4])
+    start(with_columns, later_tile)
 
     @pl.loop(1, nt - 1)
     def _(lt):
         tile_main(lt)
+
+    @pl.when(first_tile)
+    def _():
+        meet()
+        start(with_rows)
+        start(with_columns)
 
     zat = [[0, 0, 0], [0, 0, 0]]
     at = [0, 0]
@@ -514,16 +547,22 @@
                 else:
                     to = ((s - 1) * r + t) * n
                     outs[lev][to:to + n] = x
-    for dz in (1, -1):
-        side = int(dz > 0)
-        send(steps_of(0, 0, dz), ZS.at[side], ZR.at[side])
+    start(with_sections)
 
     def wait_all(which):
-        for steps, copy in sent:
+        for steps, dst, copy in sent:
             if which(steps):
                 @pl.when(exists({a: -d for a, d in steps.items()}))
                 def _():
                     copy.wait_recv()
+
+    wait_all(lambda s: "gx" not in s and "gy" not in s)
+    for lev in range(3):
+        o, n, r = outs[lev], rw[lev], tiles[lev]
+        cnt = HI[lev] * r * n
+        o[0:cnt] = o[0:cnt] + ZR[1, zat[1][lev]:zat[1][lev] + cnt]
+        cnt, start = r * n, (m[lev] - 1) * r * n
+        o[start:start + cnt] = o[start:start + cnt] + ZR[0, zat[0][lev]:zat[0][lev] + cnt]
 
     wait_all(lambda s: "gx" not in s and "gy" in s)
     for lev in range(3):
@@ -628,15 +667,7 @@
                     DS[at + 1 + mm:at + 1 + mm + h])
                 add_columns(lev, lambda t: pl.ds((mm - 1) * pitch + t * n + y, 1), DS[at:at + 1])
 
-    wait_all(lambda s: "gx" not in s and "gy" not in s)
-    for lev in range(3):
-        o, n, r = outs[lev], rw[lev], tiles[lev]
-        cnt = HI[lev] * r * n
-        o[0:cnt] = o[0:cnt] + ZR[1, zat[1][lev]:zat[1][lev] + cnt]
-        cnt, start = r * n, (m[lev] - 1) * r * n
-        o[start:start + cnt] = o[start:start + cnt] + ZR[0, zat[0][lev]:zat[0][lev] + cnt]
-
-    for steps, copy in sent:
+    for steps, dst, copy in sent:
         @pl.when(exists(steps))
         def _():
             copy.wait_send()

time: 10.9 us -> 10.6 us (0.972)
  Pallas kernels: 10.1 us -> 9.85 us
    pallas_call x1, Pallas kernels: 9.26 us -> 8.98 us  [on_device(): pl.pallas_call(functools.partial(kernel, sizes, (nz, ny, nt)), out_shape=...]
where the time goes in v2:
time: 10.6 us; the launch traced here: 10.5 us
  Pallas kernels  9.85 us (93%)
  between operations  0.64 us (6%)
    pallas_call x1, Pallas kernels, on_device(): pl.pallas_call(functools.partial(kernel, sizes, (nz, ny, nt)), out_shape=...  8.98 us
    pallas_call x1, Pallas kernels, on_device(): pl.pallas_call(write_out, out_shape=tuple((jax.ShapeDtypeStruct((nz >> l,...  0.86 us

profile of v2, /device:TPU:0, one launch (start us, length us, event | category | flops | bytes accessed | tf_op | source)
XLA Modules:
  0.0 10.5 jit_solution(9631877918596071165)
XLA Ops:
  0.6 9.0 %pyramid.1 = (f32[1024,128]{1,0:T(8,128)S(1)}, f32[128,128]{1,0:T(8,128)S(1)}, f32[16,128]{1,0:T(8,128)S(1)}) custom-call(f32[16,64,1024]{2,1,0:T(8,128)} %vol.1), custom_call_target="tpu_custom_call" | custom-call | tf_op jit(solution)/shard_map/pyramid/pallas_call | solution.py:714
  9.6 0.9 %write_out.1 = (f32[8,32,512]{2,1,0:T(8,128)}, f32[4,16,256]{2,1,0:T(8,128)}, f32[2,8,128]{2,1,0:T(8,128)}) custom-call(f32[8,4,32,128]{3,2,1,0:T(8,128)S(1)} %bitcast.3, f32[4,2,16,128]{3,2,1,0:T(8,128)S(1)} %bitcast.4, f32[2,1,8,128]{3,2,1,0:T(8,128)S(1)} %bitcast.5), custom_call_target="tpu_custom_call" | custom-call | tf_op jit(solution)/shard_map/write_out/pallas_call | solution.py:737

commit v3 on v2

--- a/solution.py
+++ b/solution.py
@@ -47,23 +47,28 @@
 
 
 class Rows:
-    def __init__(self, m, tiles):
+    def __init__(self, m, tiles, up):
+        count = HI if up else (1, 1, 1)
         self.own, at = [], 0
         for lev in range(3):
             self.own.append(at)
-            at += HI[lev] * tiles[lev] * m[lev]
+            at += count[lev] * tiles[lev] * m[lev]
         self.n_own = -(-at // 8) * 8
         self.hi, at = [], self.n_own
         for lev in range(3):
             self.hi.append(at)
-            at += HI[lev] * tiles[lev] * HI[lev]
+            at += count[lev] * tiles[lev] * HI[lev]
         self.n_hi = -(-(at - self.n_own) // 8) * 8
         self.lo, at = [], self.n_own + self.n_hi
         for lev in range(3):
             self.lo.append(at)
-            at += HI[lev] * tiles[lev]
+            at += count[lev] * tiles[lev]
         self.n_lo = -(-(at - self.n_own - self.n_hi) // 8) * 8
         self.total = self.n_own + self.n_hi + self.n_lo
+
+
+def aligned(i, n):
+    return i * n if isinstance(i, int) else pl.multiple_of(i * n, n)
 
 
 def conv(load):
@@ -85,8 +90,8 @@
 
 def kernel(sizes, dims, vol, out1, out2, out3,
            v, Z, A2Z, A3Z, EA1, EA2, EG2, EG3, YG, YX, LX1, LX2, LX3,
-           W1, W2, W3, WG, DS, YS, YR, XS, XR, ZS, ZR,
-           load_sem, send_sem, recv_sem):
+           W1, W2, W3, WG, DS, YS, YR, XS, XR, XQ, ZS, ZR,
+           load_sem, send_sem, recv_sem, ready):
     nz, ny, nt = dims
     m = [nz >> 1, nz >> 2, nz >> 3]
     rw = [ny >> 1, ny >> 2, ny >> 3]
@@ -94,7 +99,7 @@
     tiles = [nt >> 1, nt >> 2, nt >> 3]
     ZP, P2, P3 = ny + 3, rw[0] + 3, rw[1] + 3
     E1P, E2P = 2 * ext[1] + 3, 2 * ext[2] + 3
-    rowmap = Rows(m, tiles)
+    rowmaps = Rows(m, tiles, False), Rows(m, tiles, True)
     outs = (out1, out2, out3)
 
     idx = {a: lax.axis_index(a) for a in AXES}
@@ -116,6 +121,19 @@
     def flag(a, d):
         return jnp.where(has[a, d], 1.0, 0.0).astype(f32)
 
+    def upward(steps):
+        return steps.get("gx") == 1 and steps.get("gy") == 1
+
+    def downward(steps):
+        return steps.get("gx") == -1 and steps.get("gy") == -1
+
+    across = jnp.logical_and(idx["gy"] == sizes["gy"] // 2 - 1, has["gy", 1])
+    below_across = idx["gy"] == sizes["gy"] // 2
+
+    def near_by(steps):
+        far = across if upward(steps) else below_across
+        return jnp.logical_and(exists(steps), jnp.logical_not(far))
+
     fz_lo, fz_hi = flag("gz", -1), flag("gz", 1)
     fy_lo, fy_hi = flag("gy", -1), flag("gy", 1)
     fx_lo, fx_hi = flag("gx", -1), flag("gx", 1)
@@ -129,18 +147,23 @@
 
     low, high = 8, ny - 16
     loads = []
-    for i, (r0, rn) in enumerate(((0, low), (high, 16), (low, high - low))):
-        c = pltpu.make_async_copy(
-            vol.at[:, pl.ds(r0, rn), :], v.at[:, pl.ds(r0, rn), :], load_sem.at[i])
-        c.start()
-        loads.append(c)
+    tops, rest = ((0, low), (high, 16)), ((low, high - low),)
+    ends_first = ((0, 1), (nt - 1, 1), (1, nt - 2))
+    for rows, spans in ((tops, ends_first), (rest, ends_first)):
+        for c0, cn in spans:
+            for r0, rn in rows:
+                here = (slice(None), pl.ds(r0, rn), pl.ds(c0 * LANES, cn * LANES))
+                c = pltpu.make_async_copy(vol.at[here], v.at[here], load_sem.at[len(loads)])
+                c.start()
+                loads.append(c)
     for p in peers:
+        if downward(p):
+            continue
+
         @pl.when(exists(p))
         def _():
             pl.semaphore_signal(barrier, inc=1, device_id=device(p), device_id_type=MESH)
 
-    segments = ((0, 0, rowmap.n_own), (1, rowmap.n_own, rowmap.n_hi),
-                (-1, rowmap.n_own + rowmap.n_hi, rowmap.n_lo))
     sent = []
 
     def message(steps, src, dst):
@@ -158,7 +181,9 @@
                 slot = 5 + 3 * (dy < 0) + (0, 1, -1).index(dz)
                 message(steps_of(dx, dy, dz), XS.at[5], XR.at[int(dx < 0), slot])
     for dy in (-1, 1):
-        for dz, at, n in segments:
+        rowmap = rowmaps[int(dy > 0)]
+        for dz, at, n in ((0, 0, rowmap.n_own), (1, rowmap.n_own, rowmap.n_hi),
+                          (-1, rowmap.n_own + rowmap.n_hi, rowmap.n_lo)):
             message(steps_of(0, dy, dz), YS.at[int(dy > 0), pl.ds(at, n)],
                     YR.at[int(dy < 0), pl.ds(at, n)])
     for dx in (-1, 1):
@@ -170,10 +195,27 @@
         side = int(dz > 0)
         message(steps_of(0, 0, dz), ZS.at[side], ZR.at[side])
 
+    relayed = []
+    for at, (steps, dst, copy) in enumerate(sent):
+        if upward(steps):
+            onward = {a: d for a, d in steps.items() if a != "gx"}
+            ok = jnp.logical_and(jnp.logical_and(exists(onward), has["gx", -1]), across)
+            relayed.append((ok, pltpu.make_async_remote_copy(
+                src_ref=XQ, dst_ref=dst, send_sem=send_sem.at[at], recv_sem=recv_sem.at[at],
+                device_id=device(onward), device_id_type=MESH)))
+    passing = pltpu.make_async_remote_copy(
+        src_ref=XS.at[5], dst_ref=XQ, send_sem=send_sem.at[len(sent)],
+        recv_sem=recv_sem.at[len(sent)], device_id=device({"gx": 1}), device_id_type=MESH)
+    passes = jnp.logical_and(across, has["gx", 1])
+    passed = jnp.logical_and(across, has["gx", -1])
+
+    def goes(steps):
+        return near_by(steps) if upward(steps) else exists(steps)
+
     def start(which, when=None):
         for steps, dst, copy in sent:
             if which(steps):
-                ok = exists(steps)
+                ok = goes(steps)
 
                 @pl.when(ok if when is None else jnp.logical_and(ok, when))
                 def _():
@@ -184,8 +226,11 @@
         def _():
             dst[...] = jnp.zeros(dst.shape, f32)
 
+    def with_corners(steps):
+        return "gy" in steps and "gx" in steps and not upward(steps)
+
     def with_rows(steps):
-        return "gy" in steps
+        return "gy" in steps and "gx" not in steps
 
     def with_columns(steps):
         return "gx" in steps and "gy" not in steps
@@ -194,7 +239,15 @@
         return "gx" not in steps and "gy" not in steps
 
     def meet():
-        pl.semaphore_wait(barrier, sum(exists(p).astype(jnp.int32) for p in peers))
+        pl.semaphore_wait(barrier, sum(
+            exists(p).astype(jnp.int32) for p in peers if not upward(p)))
+
+    def answer():
+        for p in peers:
+            if downward(p):
+                @pl.when(near_by(p))
+                def _():
+                    pl.semaphore_signal(ready, inc=1, device_id=device(p), device_id_type=MESH)
 
     first_tile = jnp.logical_not(jnp.logical_or(has["gx", -1], has["gy", -1]))
     later_tile = jnp.logical_or(has["gx", -1], has["gy", -1])
@@ -211,9 +264,11 @@
         Z[pl.ds(i * ZP - 1, 3)] = jnp.zeros((3, LANES), f32)
     clear(Z, nt * ext[0] * ZP - 1, 1)
     for s in range(ext[1]):
-        clear(A2Z, s * P2, 1)
+        clear(A2Z.at[0], s * P2, 1)
+        clear(A2Z.at[1], s * P2, 1)
     for s in range(ext[2]):
-        clear(A3Z, s * P3, 1)
+        clear(A3Z.at[0], s * P3, 1)
+        clear(A3Z.at[1], s * P3, 1)
     EA1[...] = jnp.zeros(EA1.shape, f32)
     EA2[...] = jnp.zeros(EA2.shape, f32)
     YG[...] = jnp.zeros(YG.shape, f32)
@@ -296,7 +351,7 @@
         WG[16 * lev:16 * lev + 16] = both.astype(bf16)
 
     def z_block(lt, r, base):
-        cols = pl.ds(pl.multiple_of(lt * LANES, LANES), LANES)
+        cols = pl.ds(aligned(lt, LANES), LANES)
         x = [v[i, r:r + 8, cols] for i in range(nz)]
         for s in range(ext[0]):
             o = s - 1
@@ -311,7 +366,8 @@
         row = lax.broadcasted_iota(jnp.int32, (n, LANES), 0)
         return jnp.where(row == 0, fz_lo, jnp.where(row > mz, fz_hi, 1.0))
 
-    def edge(lt, base):
+    def edge(lt, base, slot):
+        ea1, ea2, yg = EA1.at[slot], EA2.at[slot], YG.at[slot]
         src = {}
 
         def zy(y):
@@ -324,46 +380,47 @@
         a2z = {}
         for k, e in enumerate(rows1):
             x = partial_conv(zy, e, 0, ny)
-            EA1[k * E1P + 3:k * E1P + 3 + ext[0]] = x
+            ea1[k * E1P + 3:k * E1P + 3 + ext[0]] = x
             if e == -1:
-                YG[0:ext[0]] = x
+                yg[0:ext[0]] = x
             elif e == n1:
-                YG[16:16 + ext[0]] = x
+                yg[16:16 + ext[0]] = x
         for k, e in enumerate(rows1):
-            a2z[e] = conv(lambda j: EA1[pl.ds(k * E1P + 2 + j, ext[1], 2)]) * f2
-        at = pl.multiple_of(lt * 16, 8)
+            a2z[e] = conv(lambda j: ea1[pl.ds(k * E1P + 2 + j, ext[1], 2)]) * f2
+        at = aligned(lt, 16)
         EG2[pl.ds(at, ext[1])] = a2z[-1]
         EG2[pl.ds(at + 8, ext[1])] = a2z[n1]
         rows2 = [-1, 0, n2 - 2, n2 - 1, n2, n2 + 1]
         a3z = {}
         for k, e in enumerate(rows2):
             x = partial_conv(lambda i: a2z[i], e, -1, n1 + 1)
-            EA2[k * E2P + 3:k * E2P + 3 + ext[1]] = x
+            ea2[k * E2P + 3:k * E2P + 3 + ext[1]] = x
             if e in (-1, n2, n2 + 1):
                 r = 32 + 8 * (0, n2, n2 + 1).index(max(e, 0))
-                YG[r:r + ext[1]] = x
+                yg[r:r + ext[1]] = x
         for k, e in enumerate(rows2):
-            a3z[e] = conv(lambda j: EA2[pl.ds(k * E2P + 2 + j, ext[2], 2)]) * f3
+            a3z[e] = conv(lambda j: ea2[pl.ds(k * E2P + 2 + j, ext[2], 2)]) * f3
         EG3[pl.ds(at, ext[2])] = a3z[-1]
         EG3[pl.ds(at + 8, ext[2])] = a3z[n2]
         for k, e in enumerate((-1, n3, n3 + 1)):
             x = partial_conv(lambda i: a3z[i], e, -1, n2 + 2)
-            YG[64 + 8 * k:64 + 8 * k + ext[2]] = x
-        cols = pl.ds(pl.multiple_of(lt * LANES, LANES), LANES)
+            yg[64 + 8 * k:64 + 8 * k + ext[2]] = x
+        cols = pl.ds(aligned(lt, LANES), LANES)
         for lev in range(3):
-            hi, mid = split2(YG[32 * lev:32 * lev + 32])
+            hi, mid = split2(yg[32 * lev:32 * lev + 32])
             YX[64 * lev:64 * lev + 32, cols] = hi
             YX[64 * lev + 32:64 * lev + 64, cols] = mid
 
     order3 = list(range(1, ext[2])) + [0]
 
-    def main(lt, base):
-        cols = pl.ds(pl.multiple_of(lt * LANES, LANES), LANES)
-        at = pl.multiple_of(lt * 16, 8)
-        A2Z[pl.ds(1, ext[1], P2)] = EG2[pl.ds(at, ext[1])] * fy_lo
-        A2Z[pl.ds(rw[0] + 2, ext[1], P2)] = EG2[pl.ds(at + 8, ext[1])] * fy_hi
-        A3Z[pl.ds(1, ext[2], P3)] = EG3[pl.ds(at, ext[2])] * fy_lo
-        A3Z[pl.ds(rw[1] + 2, ext[2], P3)] = EG3[pl.ds(at + 8, ext[2])] * fy_hi
+    def main(lt, base, slot):
+        a2, a3 = A2Z.at[slot], A3Z.at[slot]
+        cols = pl.ds(aligned(lt, LANES), LANES)
+        at = aligned(lt, 16)
+        a2[pl.ds(1, ext[1], P2)] = EG2[pl.ds(at, ext[1])] * fy_lo
+        a2[pl.ds(rw[0] + 2, ext[1], P2)] = EG2[pl.ds(at + 8, ext[1])] * fy_hi
+        a3[pl.ds(1, ext[2], P3)] = EG3[pl.ds(at, ext[2])] * fy_lo
+        a3[pl.ds(rw[1] + 2, ext[2], P3)] = EG3[pl.ds(at + 8, ext[2])] * fy_hi
 
         def reduce_sections(x, lev):
             for s in range(ext[lev]):
@@ -386,11 +443,11 @@
                 LX1[ext[0] * rw[0] + r:ext[0] * rw[0] + r + 16, cols] = mid
                 x.append(y)
             for s, y in reduce_sections(x, 1):
-                A2Z[s * P2 + q + 2:s * P2 + q + 18] = y
+                a2[s * P2 + q + 2:s * P2 + q + 18] = y
         for q in range(0, rw[1], 16):
             x = []
             for s in range(ext[1]):
-                half = [conv(lambda j: A2Z[pl.ds(s * P2 + 2 * (q + h) + 2 + j, 8, 2)])
+                half = [conv(lambda j: a2[pl.ds(s * P2 + 2 * (q + h) + 2 + j, 8, 2)])
                         for h in (0, 8)]
                 y = jnp.concatenate(half, axis=0)
                 hi, mid = split2(y)
@@ -399,10 +456,10 @@
                 LX2[ext[1] * rw[1] + r:ext[1] * rw[1] + r + 16, cols] = mid
                 x.append(y)
             for s, y in reduce_sections(x, 2):
-                A3Z[s * P3 + q + 2:s * P3 + q + 18] = y
+                a3[s * P3 + q + 2:s * P3 + q + 18] = y
         x = {}
         for s in range(ext[2]):
-            x[s] = conv(lambda j: A3Z[pl.ds(s * P3 + 2 + j, 8, 2)])
+            x[s] = conv(lambda j: a3[pl.ds(s * P3 + 2 + j, 8, 2)])
         n = LX3.shape[0] // 2
         for i in range(0, n // 8, 2):
             pair = [x[order3[k]] if k < ext[2] else zero for k in (i, i + 1)]
@@ -460,21 +517,55 @@
                 start += n
             yield out
 
-    for c in loads[0:2]:
-        c.wait()
-
-    @pl.loop(0, nt)
-    def _(lt):
+    def tile_edge(lt, slot):
         base = lt * (ext[0] * ZP)
         for r in [0] + list(range(high, ny, 8)):
             z_block(lt, r, base)
-        edge(lt, base)
+        edge(lt, base, slot)
+
+    for c in loads[0:4]:
+        c.wait()
+    tile_edge(0, 0)
+    tile_edge(nt - 1, 1)
+    XS[5] = next(spill_columns([[(lev, YX, 64 * lev, 32, 32) for lev in range(3)]]))
+    for c in loads[4:6]:
+        c.wait()
+
+    @pl.loop(0, (nt - 2) // 2)
+    def _(i):
+        tile_edge(1 + 2 * i, 0)
+        tile_edge(2 + 2 * i, 1)
+
+    def first_sends():
+        meet()
+        start(with_corners)
+
+        @pl.when(passes)
+        def _():
+            passing.start()
+        answer()
+
+    @pl.when(later_tile)
+    def _():
+        first_sends()
+
+    def tile_main(lt, slot):
+        base = lt * (ext[0] * ZP)
+        for r in range(low, high, 8):
+            z_block(lt, r, base)
+        main(lt, base, slot)
+
+    for c in loads[6:8]:
+        c.wait()
+    tile_main(0, 0)
+    tile_main(nt - 1, 1)
 
     for lev in range(3):
         for t, d in columns(lev, lambda cols: YX[64 * lev:64 * lev + 64, cols]):
             DS[32 * t:32 * t + 32] = d
             e, mm, h = 16 if lev == 0 else 8, m[lev], HI[lev]
             for side in (0, 1):
+                rowmap = rowmaps[side]
                 for k in range(h if side else 1):
                     r = 32 * t + e * (side + k)
                     slot = k * tiles[lev] + t
@@ -484,25 +575,10 @@
                     YS[side, to:to + h] = DS[r + 1 + mm:r + 1 + mm + h]
                     to = rowmap.lo[lev] + slot
                     YS[side, to:to + 1] = DS[r:r + 1]
-    spill = spill_columns([[(lev, YX, 64 * lev, 32, 32) for lev in range(3)]])
-    XS[5] = next(spill)
 
     @pl.when(later_tile)
     def _():
-        meet()
         start(with_rows)
-
-    loads[2].wait()
-
-    def tile_main(lt):
-        base = lt * (ext[0] * ZP)
-        for r in range(low, high, 8):
-            z_block(lt, r, base)
-        main(lt, base)
-
-    @pl.loop(0, 2)
-    def _(i):
-        tile_main(i * (nt - 1))
 
     o1, o2 = ext[0] * rw[0], ext[1] * rw[1]
     o3 = LX3.shape[0] // 2
@@ -516,15 +592,32 @@
         XS[i] = x
     start(with_columns, later_tile)
 
-    @pl.loop(1, nt - 1)
-    def _(lt):
-        tile_main(lt)
+    loads[8].wait()
+
+    @pl.loop(0, (nt - 2) // 2)
+    def _(i):
+        tile_main(1 + 2 * i, 0)
+        tile_main(2 + 2 * i, 1)
 
     @pl.when(first_tile)
     def _():
-        meet()
+        first_sends()
         start(with_rows)
         start(with_columns)
+
+    @pl.when(passed)
+    def _():
+        passing.wait_recv()
+    for ok, copy in relayed:
+        @pl.when(ok)
+        def _():
+            copy.start()
+    answers = sum(near_by(p).astype(jnp.int32) for p in peers if upward(p))
+
+    @pl.when(answers > 0)
+    def _():
+        pl.semaphore_wait(ready, answers)
+    start(upward)
 
     zat = [[0, 0, 0], [0, 0, 0]]
     at = [0, 0]
@@ -564,11 +657,25 @@
         cnt, start = r * n, (m[lev] - 1) * r * n
         o[start:start + cnt] = o[start:start + cnt] + ZR[0, zat[0][lev]:zat[0][lev] + cnt]
 
-    wait_all(lambda s: "gx" not in s and "gy" in s)
+    for steps, dst, copy in sent:
+        @pl.when(goes(steps))
+        def _():
+            copy.wait_send()
+
+    @pl.when(passes)
+    def _():
+        passing.wait_send()
+    for ok, copy in relayed:
+        @pl.when(ok)
+        def _():
+            copy.wait_send()
+
+    wait_all(lambda s: "gx" in s or "gy" in s)
     for lev in range(3):
         o, n, r, mm = outs[lev], rw[lev], tiles[lev], m[lev]
         pitch = r * n
         for side in (0, 1):
+            rowmap = rowmaps[1 - side]
             for k in range(1 if side else HI[lev]):
                 y = n - 1 if side else k
                 for t in range(r):
@@ -587,7 +694,6 @@
                     here = pl.ds((mm - 1) * pitch + t * n + y, 1)
                     o[here] = o[here] + down
 
-    wait_all(lambda s: "gx" in s and "gy" not in s)
 
     def unpack(lo, hi):
         x = jnp.concatenate([lo, jnp.zeros((LANES - 16, LANES), f32), hi], axis=0)
@@ -630,7 +736,6 @@
         section(lev, m[lev] - 1, x[at:at + rw[lev]])
         at += rw[lev]
 
-    wait_all(lambda s: "gx" in s and "gy" in s)
     lane96 = lane % 32
     kind_s = jnp.where(lane < 32, lane % 16, lane % 8)
     is_up = lane96 >= jnp.where(lane < 32, 16, 8)
@@ -667,11 +772,6 @@
                     DS[at + 1 + mm:at + 1 + mm + h])
                 add_columns(lev, lambda t: pl.ds((mm - 1) * pitch + t * n + y, 1), DS[at:at + 1])
 
-    for steps, dst, copy in sent:
-        @pl.when(exists(steps))
-        def _():
-            copy.wait_send()
-
 
 def write_out(a1, a2, a3, out1, out2, out3, sem):
     copies = []
@@ -695,7 +795,7 @@
     ext = [m[l] + 1 + HI[l] for l in range(3)]
     ZP, P2, P3 = ny + 3, rw[0] + 3, rw[1] + 3
     E1P, E2P = 2 * ext[1] + 3, 2 * ext[2] + 3
-    rowmap = Rows(m, tiles)
+    rowmap = Rows(m, tiles, True)
     n3 = -(-ext[2] * rw[2] // 16) * 16
     zrows = sum(HI[l] * tiles[l] * rw[l] for l in range(3))
     dma = pltpu.SemaphoreType.DMA
@@ -704,6 +804,9 @@
 
     def flat(n):
         return V((-(-n // 8) * 8, LANES), f32)
+
+    def two(n):
+        return V((2, -(-n // 8) * 8, LANES), f32)
 
     def weights(lev):
         found = blocks_of(lev, nt)
@@ -718,16 +821,16 @@
         out_specs=(vmem, vmem, vmem),
         scratch_shapes=[
             V((nz, ny, nx), f32),
-            flat(nt * ext[0] * ZP), flat(ext[1] * P2), flat(ext[2] * P3),
-            flat(11 * E1P), flat(6 * E2P), flat(16 * nt), flat(16 * nt), flat(96),
+            flat(nt * ext[0] * ZP), two(ext[1] * P2), two(ext[2] * P3),
+            two(11 * E1P), two(6 * E2P), flat(16 * nt), flat(16 * nt), two(96),
             V((192, nx), bf16),
             V((2 * ext[0] * rw[0], nx), bf16), V((2 * ext[1] * rw[1], nx), bf16),
             V((2 * n3, nx), bf16),
             weights(0), weights(1), weights(2), V((48, LANES), bf16),
             flat(LANES), V((2, rowmap.total, LANES), f32), V((2, rowmap.total, LANES), f32),
-            V((6, 8, LANES), f32), V((2, 11, 8, LANES), f32),
+            V((6, 8, LANES), f32), V((2, 11, 8, LANES), f32), V((8, LANES), f32),
             V((2, zrows, LANES), f32), V((2, zrows, LANES), f32),
-            dma((3,)), dma((26,)), dma((26,)),
+            dma((9,)), dma((27,)), dma((27,)), pltpu.SemaphoreType.REGULAR,
         ],
         compiler_params=pltpu.CompilerParams(
             collective_id=0, has_side_effects=True, vmem_limit_bytes=40 << 20),

time: 10.6 us -> 10.5 us (level)
  no operation moved by 1% of the time
where the time goes in v3:
time: 10.5 us; the launch traced here: 10.4 us
  Pallas kernels  9.75 us (93%)
  between operations  0.64 us (6%)
    pallas_call x1, Pallas kernels, on_device(): pl.pallas_call(functools.partial(kernel, sizes, (nz, ny, nt)), out_shape=...  8.88 us
    pallas_call x1, Pallas kernels, on_device(): pl.pallas_call(write_out, out_shape=tuple((jax.ShapeDtypeStruct((nz >> l,...  0.86 us

profile of v3, /device:TPU:0, one launch (start us, length us, event | category | flops | bytes accessed | tf_op | source)
XLA Modules:
  0.0 10.4 jit_solution(11003671835716612229)
XLA Ops:
  0.6 8.9 %pyramid.1 = (f32[1024,128]{1,0:T(8,128)S(1)}, f32[128,128]{1,0:T(8,128)S(1)}, f32[16,128]{1,0:T(8,128)S(1)}) custom-call(f32[16,64,1024]{2,1,0:T(8,128)} %vol.1), custom_call_target="tpu_custom_call" | custom-call | tf_op jit(solution)/shard_map/pyramid/pallas_call | solution.py:817
  9.5 0.9 %write_out.1 = (f32[8,32,512]{2,1,0:T(8,128)}, f32[4,16,256]{2,1,0:T(8,128)}, f32[2,8,128]{2,1,0:T(8,128)}) custom-call(f32[8,4,32,128]{3,2,1,0:T(8,128)S(1)} %bitcast.3, f32[4,2,16,128]{3,2,1,0:T(8,128)S(1)} %bitcast.4, f32[2,1,8,128]{3,2,1,0:T(8,128)S(1)} %bitcast.5), custom_call_target="tpu_custom_call" | custom-call | tf_op jit(solution)/shard_map/write_out/pallas_call | solution.py:840

commit v4 on v3

--- a/solution.py
+++ b/solution.py
@@ -47,22 +47,21 @@
 
 
 class Rows:
-    def __init__(self, m, tiles, up):
-        count = HI if up else (1, 1, 1)
+    def __init__(self, m, tiles):
         self.own, at = [], 0
         for lev in range(3):
             self.own.append(at)
-            at += count[lev] * tiles[lev] * m[lev]
+            at += HI[lev] * tiles[lev] * m[lev]
         self.n_own = -(-at // 8) * 8
         self.hi, at = [], self.n_own
         for lev in range(3):
             self.hi.append(at)
-            at += count[lev] * tiles[lev] * HI[lev]
+            at += HI[lev] * tiles[lev] * HI[lev]
         self.n_hi = -(-(at - self.n_own) // 8) * 8
         self.lo, at = [], self.n_own + self.n_hi
         for lev in range(3):
             self.lo.append(at)
-            at += count[lev] * tiles[lev]
+            at += HI[lev] * tiles[lev]
         self.n_lo = -(-(at - self.n_own - self.n_hi) // 8) * 8
         self.total = self.n_own + self.n_hi + self.n_lo
 
@@ -90,8 +89,8 @@
 
 def kernel(sizes, dims, vol, out1, out2, out3,
            v, Z, A2Z, A3Z, EA1, EA2, EG2, EG3, YG, YX, LX1, LX2, LX3,
-           W1, W2, W3, WG, DS, YS, YR, XS, XR, XQ, ZS, ZR,
-           load_sem, send_sem, recv_sem, ready):
+           W1, W2, W3, WG, DS, YS, YR, XS, XR, ZS, ZR,
+           load_sem, send_sem, recv_sem):
     nz, ny, nt = dims
     m = [nz >> 1, nz >> 2, nz >> 3]
     rw = [ny >> 1, ny >> 2, ny >> 3]
@@ -99,7 +98,7 @@
     tiles = [nt >> 1, nt >> 2, nt >> 3]
     ZP, P2, P3 = ny + 3, rw[0] + 3, rw[1] + 3
     E1P, E2P = 2 * ext[1] + 3, 2 * ext[2] + 3
-    rowmaps = Rows(m, tiles, False), Rows(m, tiles, True)
+    rowmap = Rows(m, tiles)
     outs = (out1, out2, out3)
 
     idx = {a: lax.axis_index(a) for a in AXES}
@@ -120,19 +119,6 @@
 
     def flag(a, d):
         return jnp.where(has[a, d], 1.0, 0.0).astype(f32)
-
-    def upward(steps):
-        return steps.get("gx") == 1 and steps.get("gy") == 1
-
-    def downward(steps):
-        return steps.get("gx") == -1 and steps.get("gy") == -1
-
-    across = jnp.logical_and(idx["gy"] == sizes["gy"] // 2 - 1, has["gy", 1])
-    below_across = idx["gy"] == sizes["gy"] // 2
-
-    def near_by(steps):
-        far = across if upward(steps) else below_across
-        return jnp.logical_and(exists(steps), jnp.logical_not(far))
 
     fz_lo, fz_hi = flag("gz", -1), flag("gz", 1)
     fy_lo, fy_hi = flag("gy", -1), flag("gy", 1)
@@ -157,13 +143,12 @@
                 c.start()
                 loads.append(c)
     for p in peers:
-        if downward(p):
-            continue
-
         @pl.when(exists(p))
         def _():
             pl.semaphore_signal(barrier, inc=1, device_id=device(p), device_id_type=MESH)
 
+    segments = ((0, 0, rowmap.n_own), (1, rowmap.n_own, rowmap.n_hi),
+                (-1, rowmap.n_own + rowmap.n_hi, rowmap.n_lo))
     sent = []
 
     def message(steps, src, dst):
@@ -181,9 +166,7 @@
                 slot = 5 + 3 * (dy < 0) + (0, 1, -1).index(dz)
                 message(steps_of(dx, dy, dz), XS.at[5], XR.at[int(dx < 0), slot])
     for dy in (-1, 1):
-        rowmap = rowmaps[int(dy > 0)]
-        for dz, at, n in ((0, 0, rowmap.n_own), (1, rowmap.n_own, rowmap.n_hi),
-                          (-1, rowmap.n_own + rowmap.n_hi, rowmap.n_lo)):
+        for dz, at, n in segments:
             message(steps_of(0, dy, dz), YS.at[int(dy > 0), pl.ds(at, n)],
                     YR.at[int(dy < 0), pl.ds(at, n)])
     for dx in (-1, 1):
@@ -195,27 +178,10 @@
         side = int(dz > 0)
         message(steps_of(0, 0, dz), ZS.at[side], ZR.at[side])
 
-    relayed = []
-    for at, (steps, dst, copy) in enumerate(sent):
-        if upward(steps):
-            onward = {a: d for a, d in steps.items() if a != "gx"}
-            ok = jnp.logical_and(jnp.logical_and(exists(onward), has["gx", -1]), across)
-            relayed.append((ok, pltpu.make_async_remote_copy(
-                src_ref=XQ, dst_ref=dst, send_sem=send_sem.at[at], recv_sem=recv_sem.at[at],
-                device_id=device(onward), device_id_type=MESH)))
-    passing = pltpu.make_async_remote_copy(
-        src_ref=XS.at[5], dst_ref=XQ, send_sem=send_sem.at[len(sent)],
-        recv_sem=recv_sem.at[len(sent)], device_id=device({"gx": 1}), device_id_type=MESH)
-    passes = jnp.logical_and(across, has["gx", 1])
-    passed = jnp.logical_and(across, has["gx", -1])
-
-    def goes(steps):
-        return near_by(steps) if upward(steps) else exists(steps)
-
     def start(which, when=None):
         for steps, dst, copy in sent:
             if which(steps):
-                ok = goes(steps)
+                ok = exists(steps)
 
                 @pl.when(ok if when is None else jnp.logical_and(ok, when))
                 def _():
@@ -227,7 +193,7 @@
             dst[...] = jnp.zeros(dst.shape, f32)
 
     def with_corners(steps):
-        return "gy" in steps and "gx" in steps and not upward(steps)
+        return "gy" in steps and "gx" in steps
 
     def with_rows(steps):
         return "gy" in steps and "gx" not in steps
@@ -239,15 +205,7 @@
         return "gx" not in steps and "gy" not in steps
 
     def meet():
-        pl.semaphore_wait(barrier, sum(
-            exists(p).astype(jnp.int32) for p in peers if not upward(p)))
-
-    def answer():
-        for p in peers:
-            if downward(p):
-                @pl.when(near_by(p))
-                def _():
-                    pl.semaphore_signal(ready, inc=1, device_id=device(p), device_id_type=MESH)
+        pl.semaphore_wait(barrier, sum(exists(p).astype(jnp.int32) for p in peers))
 
     first_tile = jnp.logical_not(jnp.logical_or(has["gx", -1], has["gy", -1]))
     later_tile = jnp.logical_or(has["gx", -1], has["gy", -1])
@@ -527,7 +485,6 @@
         c.wait()
     tile_edge(0, 0)
     tile_edge(nt - 1, 1)
-    XS[5] = next(spill_columns([[(lev, YX, 64 * lev, 32, 32) for lev in range(3)]]))
     for c in loads[4:6]:
         c.wait()
 
@@ -535,19 +492,6 @@
     def _(i):
         tile_edge(1 + 2 * i, 0)
         tile_edge(2 + 2 * i, 1)
-
-    def first_sends():
-        meet()
-        start(with_corners)
-
-        @pl.when(passes)
-        def _():
-            passing.start()
-        answer()
-
-    @pl.when(later_tile)
-    def _():
-        first_sends()
 
     def tile_main(lt, slot):
         base = lt * (ext[0] * ZP)
@@ -555,17 +499,11 @@
             z_block(lt, r, base)
         main(lt, base, slot)
 
-    for c in loads[6:8]:
-        c.wait()
-    tile_main(0, 0)
-    tile_main(nt - 1, 1)
-
     for lev in range(3):
         for t, d in columns(lev, lambda cols: YX[64 * lev:64 * lev + 64, cols]):
             DS[32 * t:32 * t + 32] = d
             e, mm, h = 16 if lev == 0 else 8, m[lev], HI[lev]
             for side in (0, 1):
-                rowmap = rowmaps[side]
                 for k in range(h if side else 1):
                     r = 32 * t + e * (side + k)
                     slot = k * tiles[lev] + t
@@ -575,10 +513,18 @@
                     YS[side, to:to + h] = DS[r + 1 + mm:r + 1 + mm + h]
                     to = rowmap.lo[lev] + slot
                     YS[side, to:to + 1] = DS[r:r + 1]
+    XS[5] = next(spill_columns([[(lev, YX, 64 * lev, 32, 32) for lev in range(3)]]))
 
     @pl.when(later_tile)
     def _():
+        meet()
+        start(with_corners)
         start(with_rows)
+
+    for c in loads[6:8]:
+        c.wait()
+    tile_main(0, 0)
+    tile_main(nt - 1, 1)
 
     o1, o2 = ext[0] * rw[0], ext[1] * rw[1]
     o3 = LX3.shape[0] // 2
@@ -601,23 +547,10 @@
 
     @pl.when(first_tile)
     def _():
-        first_sends()
+        meet()
+        start(with_corners)
         start(with_rows)
         start(with_columns)
-
-    @pl.when(passed)
-    def _():
-        passing.wait_recv()
-    for ok, copy in relayed:
-        @pl.when(ok)
-        def _():
-            copy.start()
-    answers = sum(near_by(p).astype(jnp.int32) for p in peers if upward(p))
-
-    @pl.when(answers > 0)
-    def _():
-        pl.semaphore_wait(ready, answers)
-    start(upward)
 
     zat = [[0, 0, 0], [0, 0, 0]]
     at = [0, 0]
@@ -658,15 +591,7 @@
         o[start:start + cnt] = o[start:start + cnt] + ZR[0, zat[0][lev]:zat[0][lev] + cnt]
 
     for steps, dst, copy in sent:
-        @pl.when(goes(steps))
-        def _():
-            copy.wait_send()
-
-    @pl.when(passes)
-    def _():
-        passing.wait_send()
-    for ok, copy in relayed:
-        @pl.when(ok)
+        @pl.when(exists(steps))
         def _():
             copy.wait_send()
 
@@ -675,7 +600,6 @@
         o, n, r, mm = outs[lev], rw[lev], tiles[lev], m[lev]
         pitch = r * n
         for side in (0, 1):
-            rowmap = rowmaps[1 - side]
             for k in range(1 if side else HI[lev]):
                 y = n - 1 if side else k
                 for t in range(r):
@@ -795,7 +719,7 @@
     ext = [m[l] + 1 + HI[l] for l in range(3)]
     ZP, P2, P3 = ny + 3, rw[0] + 3, rw[1] + 3
     E1P, E2P = 2 * ext[1] + 3, 2 * ext[2] + 3
-    rowmap = Rows(m, tiles, True)
+    rowmap = Rows(m, tiles)
     n3 = -(-ext[2] * rw[2] // 16) * 16
     zrows = sum(HI[l] * tiles[l] * rw[l] for l in range(3))
     dma = pltpu.SemaphoreType.DMA
@@ -828,9 +752,9 @@
             V((2 * n3, nx), bf16),
             weights(0), weights(1), weights(2), V((48, LANES), bf16),
             flat(LANES), V((2, rowmap.total, LANES), f32), V((2, rowmap.total, LANES), f32),
-            V((6, 8, LANES), f32), V((2, 11, 8, LANES), f32), V((8, LANES), f32),
+            V((6, 8, LANES), f32), V((2, 11, 8, LANES), f32),
             V((2, zrows, LANES), f32), V((2, zrows, LANES), f32),
-            dma((9,)), dma((27,)), dma((27,)), pltpu.SemaphoreType.REGULAR,
+            dma((9,)), dma((26,)), dma((26,)),
         ],
         compiler_params=pltpu.CompilerParams(
             collective_id=0, has_side_effects=True, vmem_limit_bytes=40 << 20),

time: 10.5 us -> 10.6 us (level)
  no operation moved by 1% of the time
where the time goes in v4:
time: 10.6 us; the launch traced here: 10.4 us
  Pallas kernels  9.81 us (93%)
  between operations  0.64 us (6%)
    pallas_call x1, Pallas kernels, on_device(): pl.pallas_call(functools.partial(kernel, sizes, (nz, ny, nt)), out_shape=...  8.94 us
    pallas_call x1, Pallas kernels, on_device(): pl.pallas_call(write_out, out_shape=tuple((jax.ShapeDtypeStruct((nz >> l,...  0.86 us

profile of v4, /device:TPU:0, one launch (start us, length us, event | category | flops | bytes accessed | tf_op | source)
XLA Modules:
  0.0 10.4 jit_solution(14183233723709932437)
XLA Ops:
  0.6 8.9 %pyramid.1 = (f32[1024,128]{1,0:T(8,128)S(1)}, f32[128,128]{1,0:T(8,128)S(1)}, f32[16,128]{1,0:T(8,128)S(1)}) custom-call(f32[16,64,1024]{2,1,0:T(8,128)} %vol.1), custom_call_target="tpu_custom_call" | custom-call | tf_op jit(solution)/shard_map/pyramid/pallas_call | solution.py:741
  9.6 0.9 %write_out.1 = (f32[8,32,512]{2,1,0:T(8,128)}, f32[4,16,256]{2,1,0:T(8,128)}, f32[2,8,128]{2,1,0:T(8,128)}) custom-call(f32[8,4,32,128]{3,2,1,0:T(8,128)S(1)} %bitcast.3, f32[4,2,16,128]{3,2,1,0:T(8,128)S(1)} %bitcast.4, f32[2,1,8,128]{3,2,1,0:T(8,128)S(1)} %bitcast.5), custom_call_target="tpu_custom_call" | custom-call | tf_op jit(solution)/shard_map/write_out/pallas_call | solution.py:764
